TPU v7x, 256 devices: a whole 4x4x8 slice. The times are simulated.
256 devices in a mesh: rows: 16 (over z, core), cols: 16 (over y, x).
Axes of the slice: x: 4, y: 4, z: 8, core: 2. Of those that a mesh axis runs over, the one named last changes fastest.
Arguments:
- solved_bases: float32 [6, 128, 131072], P(None, 'cols', 'rows'), may hold values from -6 to 6
- right_bases: float32 [5, 128, 131072], P(None, 'cols', 'rows'), may hold values from -1 to 1, as said below
Outputs:
- factored_bases: float32 [5, 128, 131072], P(None, 'cols', 'rows')
Inputs may be any that keep to these rules, and one draw needn't show every extreme that they name: `right_bases`: level l is drawn with a deviation of 0.025 / sqrt(2048 * 2**l).
All inputs are finite; a program needn't handle non-finite values.
Results may differ from a plain program's by a relative error of at most 0.0001.
Values sent between devices are 32-bit elements; how exact they have to be, the bound alone decides.
No kernel may reach another device: no remote copies, remote signals or barrier semaphores. Data moves between devices by JAX's collectives and lax.ppermute only.
A program may use at most 128 MiB of HBM per device.

v0:
```python
import jax
import jax.numpy as jnp
import numpy as np
from jax import lax
from jax.experimental import pallas as pl
from jax.experimental.pallas import tpu as pltpu
from jax.sharding import Mesh
from jax.sharding import PartitionSpec as P

ROWS = ("zt", "z1", "z0", "core")
COLS = ("yh", "yl", "x")
GROUP = ("yl", "x")
LEVELS = 6
K = 128
HIGHEST = lax.Precision.HIGHEST


def dot(a, b):
    return jnp.dot(a, b, precision=HIGHEST, preferred_element_type=jnp.float32)


def dot_t(a, b):
    return lax.dot_general(a, b, (((1,), (1,)), ((), ())), precision=HIGHEST, preferred_element_type=jnp.float32)


def inverse(coupling, x_ref, r_ref):
    rows = lax.broadcasted_iota(jnp.int32, (K, K), 0)
    cols = lax.broadcasted_iota(jnp.int32, (K, K), 1)
    eye = jnp.where(rows == cols, 1.0, 0.0).astype(jnp.float32)
    matrix = eye - coupling
    square = dot(coupling, coupling)
    quick = jnp.sum(square * square) < 0.25

    @pl.when(quick)
    def _():
        x_ref[...] = eye + coupling
        r_ref[...] = square

    @pl.when(jnp.logical_not(quick))
    def _():
        size = jnp.abs(matrix)
        scale = 1.0 / (jnp.max(jnp.sum(size, axis=0)) * jnp.max(jnp.sum(size, axis=1)))
        start = matrix.T * scale
        x_ref[...] = start
        r_ref[...] = eye - dot(start, matrix)

    def size_of(r):
        return jnp.sum(r * r)

    def going(carry):
        step, size = carry
        return jnp.logical_and(step < 80, size > 1e-6)

    def refine(carry):
        step, _ = carry
        x = x_ref[...] + dot(r_ref[...], x_ref[...])
        r = eye - dot(x, matrix)
        x_ref[...] = x
        r_ref[...] = r
        return step + 1, size_of(r)

    lax.while_loop(going, refine, (jnp.int32(0), size_of(r_ref[...])))
    x_ref[...] = x_ref[...] + dot(r_ref[...], x_ref[...])


def eliminate(panel1, panel2, rest1, rest2, x_ref, r_ref):
    p1, p2 = panel1[:, :K], panel2[:, :K]
    inverse(dot(p1, p2), x_ref, r_ref)
    q1, q2 = rest1[:, :K], rest2[:, :K]
    x1 = dot(q2 - dot(q1, p2), x_ref[...])
    x2 = q1 - dot(x1, p1)
    if panel1.shape[1] == K:
        return x1, x2, None
    state = rest1[:, K:] + rest2[:, K:] - dot(x1, panel1[:, K:]) - dot(x2, panel2[:, K:])
    return x1, x2, state


def gram_kernel(a_ref, g_ref):
    right = a_ref[:, LEVELS:]
    right = jnp.transpose(right, (1, 0, 2, 3)).reshape((LEVELS - 1) * K, -1)
    for m in range(LEVELS):
        g = dot_t(a_ref[:, m].reshape(K, -1), right)
        g_ref[:, m] = g.reshape(8, 16, (LEVELS - 1) * K)


def level0_kernel(ag_ref, h_ref, x_out, panel_out, rest_out, x_ref, r_ref):
    width = (LEVELS - 1) * K
    p1, p2 = ag_ref[:, 0].reshape(K, width), ag_ref[:, 1].reshape(K, width)
    n = LEVELS - 1
    x1, x2, state = eliminate(
        p1, p2, h_ref[0, 1:].reshape(n * 16, width), h_ref[1, 1:].reshape(n * 16, width), x_ref, r_ref
    )
    state = state.reshape(n, 16, width - K)
    panel_out[...] = jnp.broadcast_to(state[0], panel_out.shape)
    rest_out[...] = state[1:]
    x_out[0] = x1.reshape(n, 16, K)
    x_out[1] = x2.reshape(n, 16, K)


def level1_kernel(side_ref, ag_ref, own_ref, other_ref, x0_ref, x_out, s_out, x_ref, r_ref):
    width = (LEVELS - 2) * K
    n = LEVELS - 2
    side = side_ref[0]
    p1 = ag_ref[pl.ds(side * 8, 8)].reshape(K, width)
    p2 = ag_ref[pl.ds((1 - side) * 8, 8)].reshape(K, width)
    x1, _, state = eliminate(
        p1, p2, own_ref[...].reshape(n * 16, width), other_ref[...].reshape(n * 16, width), x_ref, r_ref
    )
    half = (4, n + 1, 16, K)
    x_out[:4, : n + 1] = jnp.broadcast_to(x0_ref[0], half)
    x_out[4:, : n + 1] = jnp.broadcast_to(x0_ref[1], half)
    x_out[:, n + 1 :] = jnp.broadcast_to(x1.reshape(n, 16, K), (8, n, 16, K))
    s_out[...] = jnp.broadcast_to(state.reshape(n, 16, width - K), s_out.shape)


def level2_kernel(own_ref, other_ref, x_out, s_out, x_ref, r_ref):
    width = (LEVELS - 3) * K
    n = LEVELS - 3

    def rest(ref):
        return jnp.concatenate([ref[:, m].reshape(K, width) for m in range(1, n + 1)], axis=0)

    x1, _, state = eliminate(
        own_ref[:, 0].reshape(K, width), other_ref[:, 0].reshape(K, width), rest(own_ref), rest(other_ref), x_ref, r_ref
    )
    x_out[...] = x1
    s_out[...] = state


def level3_kernel(own_ref, other_ref, x_out, s_out, x_ref, r_ref):
    x1, _, state = eliminate(own_ref[:K], other_ref[:K], own_ref[K:], other_ref[K:], x_ref, r_ref)
    x_out[...] = x1
    s_out[...] = state


def level4_kernel(own_ref, other_ref, x_out, x_ref, r_ref):
    x1, _, _ = eliminate(own_ref[:K], other_ref[:K], own_ref[K:], other_ref[K:], x_ref, r_ref)
    x_out[...] = x1


def finish_kernel(a_ref, x01_ref, x2_ref, o_ref, part_ref):
    done = [a_ref[:, 0].reshape(K, -1)]

    def factor(level, i):
        if level == 2:
            return x2_ref[i * K : (i + 1) * K]
        return x01_ref[:, (LEVELS - 1) * level + i].reshape(K, K)

    for m in range(1, LEVELS):
        value = a_ref[:, m].reshape(K, -1)
        for level in range(min(m, 3)):
            value = value - dot(factor(level, m - level - 1), done[level])
        done.append(value)
        if m < 4:
            o_ref[:, m - 1] = value.reshape(16, 8, -1)
        else:
            part_ref[:, m - 4] = value.reshape(16, 8, -1)


def later_kernel(o_ref, part_ref, x3_ref, r_ref):
    base = o_ref[:, 2].reshape(K, -1)
    for i in range(2):
        value = part_ref[:, i].reshape(K, -1) - dot(x3_ref[i * K : (i + 1) * K], base)
        r_ref[:, i] = value.reshape(16, 8, -1)


def last_kernel(part_ref, x4_ref, r_ref):
    base = part_ref[:, 0]
    value = part_ref[:, 1].reshape(K, -1) - dot(x4_ref[...], base.reshape(K, -1))
    r_ref[:, 0] = base
    r_ref[:, 1] = value.reshape(16, 8, -1)


def call(kernel, outs, *args, scalar=False, flops=10**8):
    vmem = pl.BlockSpec(memory_space=pltpu.VMEM)
    specs = [vmem] * len(args)
    if scalar:
        specs[0] = pl.BlockSpec(memory_space=pltpu.SMEM)
    scratch = []
    if kernel.__name__.startswith("level"):
        scratch = [pltpu.VMEM((K, K), jnp.float32)] * 2
    shapes = [jax.ShapeDtypeStruct(s, jnp.float32) for s in outs]
    return pl.pallas_call(
        kernel,
        out_shape=shapes,
        in_specs=specs,
        out_specs=[vmem] * len(outs),
        scratch_shapes=scratch,
        compiler_params=pltpu.CompilerParams(vmem_limit_bytes=LIMIT[kernel.__name__] << 20),
        cost_estimate=pl.CostEstimate(flops=flops, bytes_accessed=10**6, transcendentals=0),
    )(*args)


def exchange(value, axis):
    return lax.ppermute(value, axis, [(0, 1), (1, 0)])


def spread(value, axes):
    return lax.all_to_all(value, axes, 0, 0, tiled=True)


def steps(solved, right):
    both = jnp.concatenate([solved, right], axis=0)
    count = both.shape[0]
    packed = both.reshape(count, 8, 16, 512).transpose(2, 0, 1, 3)
    rows = spread(packed, COLS)
    (gram,) = call(gram_kernel, [(8, LEVELS, 16, (LEVELS - 1) * K)], rows)
    gram = spread(gram, GROUP)
    h = gram.reshape(2, 4, LEVELS, 16, (LEVELS - 1) * K).sum(axis=1)

    slices = jnp.broadcast_to(h[:, 0], (8, 2, 16, (LEVELS - 1) * K))
    panels = spread(slices, GROUP)
    x0, panel, rest = call(level0_kernel, [(2, 5, 16, K), (16, 16, 4 * K), (4, 16, 4 * K)], panels, h)

    other = exchange(rest, "yh")
    panels = spread(panel, COLS)
    side = lax.axis_index("yh").astype(jnp.int32).reshape(1)
    x01, s1 = call(level1_kernel, [(8, 9, 16, K), (8, 4, 16, 3 * K)], side, panels, rest, other, x0, scalar=True)

    s1 = spread(s1, GROUP)
    other = exchange(s1, "core")
    x01 = spread(x01, GROUP)
    x2, s2 = call(level2_kernel, [(3 * K, K), (3 * K, 2 * K)], s1, other)
    other = exchange(s2, "z0")
    early, part = call(finish_kernel, [(16, 3, 8, 512), (16, 2, 8, 512)], rows, x01, x2)
    early_out = spread(early, COLS)
    x3, s3 = call(level3_kernel, [(2 * K, K), (2 * K, K)], s2, other)
    other = exchange(s3, "z1")
    (part,) = call(later_kernel, [(16, 2, 8, 512)], early, part, x3)
    (x4,) = call(level4_kernel, [(K, K)], s3, other)
    (late,) = call(last_kernel, [(16, 2, 8, 512)], part, x4)
    late, early_out = lax.optimization_barrier((late, early_out))
    late = spread(late, COLS)
    out = jnp.concatenate([early_out, late], axis=1)
    return out.transpose(1, 2, 0, 3).reshape(LEVELS - 1, 8, 8192)


def solution(mesh):
    fine = Mesh(np.array(mesh.devices).reshape(2, 2, 2, 2, 2, 2, 4), ROWS + COLS)
    spec = P(None, COLS, ROWS)
    return jax.shard_map(steps, mesh=fine, in_specs=(spec, spec), out_specs=spec, check_vma=False)


LIMIT = dict(
    gram_kernel=24,
    level0_kernel=12,
    level1_kernel=12,
    level2_kernel=12,
    level3_kernel=12,
    level4_kernel=12,
    finish_kernel=24,
    later_kernel=12,
    last_kernel=12,
)
```

profile of v0, /device:TPU:1, one launch (start us, length us, event | category | flops | bytes accessed | tf_op | source)
XLA Modules:
  0.0 201.2 jit_solution(1248197901835714431)
XLA Ops:
  2.3 43.4 %all_to_all.40.a_ref = f32[16,11,8,512]{3,2,1,0:T(8,128)S(1)} all-to-all(f32[16,11,8,512]{3,2,1,0:T(8,128)S(1)} %bitcast.16), channel_id=1, replica_groups=mesh['zt'=2,'z1'=2,'z0'=2,'core'=2,'yh'=2,'yl'=2,'x'=4] {'yh','yl','x'}, dimensions={0} | all-to-all | bytes 5767168 | tf_op jit(solution)/shard_map/all_to_all | solution.py:199
  45.7 7.2 %shard_map.28 = f32[8,6,16,640]{3,2,1,0:T(8,128)S(1)} custom-call(f32[16,11,8,512]{3,2,1,0:T(8,128)S(1)} %all_to_all.40.a_ref), custom_call_target="tpu_custom_call" | custom-call | flops 100000000 | bytes 1000000 | tf_op jit(solution)/shard_map/pallas_call | solution.py:183
  52.9 26.3 %all_to_all.41 = f32[8,6,16,640]{3,2,1,0:T(8,128)S(1)} all-to-all(f32[8,6,16,640]{3,2,1,0:T(8,128)S(1)} %shard_map.28), channel_id=1, replica_groups=mesh['zt'=2,'z1'=2,'z0'=2,'core'=2,'yh'=2,'yl'=2,'x'=4] {'yl','x'}, dimensions={0} | all-to-all | bytes 3932160 | tf_op jit(solution)/shard_map/all_to_all | solution.py:199
  79.4 11.9 %all_to_all.42.ag_ref = f32[8,2,16,640]{3,2,1,0:T(8,128)S(1)} all-to-all(f32[8,2,16,640]{3,2,1,0:T(8,128)S(1)} %broadcast_in_dim.3), channel_id=1, replica_groups=mesh['zt'=2,'z1'=2,'z0'=2,'core'=2,'yh'=2,'yl'=2,'x'=4] {'yl','x'}, dimensions={0} | all-to-all | bytes 1310720 | tf_op jit(solution)/shard_map/all_to_all | solution.py:199
  91.3 2.3 %shard_map.29 = (f32[2,5,16,128]{3,2,1,0:T(8,128)S(1)}, f32[16,16,512]{2,1,0:T(8,128)S(1)}, f32[4,16,512]{2,1,0:T(8,128)S(1)}) custom-call(f32[8,2,16,640]{3,2,1,0:T(8,128)S(1)} %all_to_all.42.ag_ref, f32[2,6,16,640]{3,2,1,0:T(8,128)S(1)} %bitcast_reduce_fusion.h_ref), custom_call_target="tpu_custom_call" | custom-call | flops 100000000 | bytes 1000000 | tf_op jit(solution)/shard_map/pallas_call | solution.py:183
  95.0 3.6 %all-to-all-start.3 = ((f32[16,16,512]{2,1,0:T(8,128)}), f32[16,16,512]{2,1,0:T(8,128)S(1)}, u32[]{:S(2)}, u32[]{:S(2)}) async-start(f32[16,16,512]{2,1,0:T(8,128)} %copy-done.3), calls=%async_computation.3 | async-start | bytes 1048576 | tf_op jit(solution)/shard_map/all_to_all | solution.py:199
  98.6 2.8 %collective-permute-start = (f32[4,16,512]{2,1,0:T(8,128)S(1)}, f32[4,16,512]{2,1,0:T(8,128)}, u32[]{:S(2)}, u32[]{:S(2)}) collective-permute-start(f32[4,16,512]{2,1,0:T(8,128)S(1)} %get-tuple-element.19.own_ref), channel_id=1, source_target_pairs={{0,8},{8,0},{1,9},{9,1},{2,10},{10,2},{3,11},{11,3},{4,12},{12,4},... | collective-permute-start | bytes 393224 | tf_op jit(solution)/shard_map/ppermute | solution.py:195
  101.4 4.2 %collective-permute-done.other_ref = f32[4,16,512]{2,1,0:T(8,128)} collective-permute-done((f32[4,16,512]{2,1,0:T(8,128)S(1)}, f32[4,16,512]{2,1,0:T(8,128)}, u32[]{:S(2)}, u32[]{:S(2)}) %collective-permute-start) | collective-permute-done | bytes 131104 | tf_op jit(solution)/shard_map/ppermute | solution.py:195
  105.6 2.3 %all-to-all-done.3.ag_ref = f32[16,16,512]{2,1,0:T(8,128)S(1)} async-done(((f32[16,16,512]{2,1,0:T(8,128)}), f32[16,16,512]{2,1,0:T(8,128)S(1)}, u32[]{:S(2)}, u32[]{:S(2)}) %all-to-all-start.3) | async-done | bytes 524320 | tf_op jit(solution)/shard_map/all_to_all | solution.py:199
  108.8 3.1 %shard_map.30 = (f32[8,9,16,128]{3,2,1,0:T(8,128)S(1)}, f32[8,4,16,384]{3,2,1,0:T(8,128)S(1)}) custom-call(s32[1]{0:T(128)} %bitcast.1.side_ref, f32[16,16,512]{2,1,0:T(8,128)S(1)} %all-to-all-done.3.ag_ref, f32[4,16,512]{2,1,0:T(8,128)S(1)} %get-tuple-element.19.own_ref, f32[4,16,512]{2,1,0:T(8,128)} %collective-permute-done.other_ref, ...), custom_call_target="tpu_custom_call" | custom-call | flops 100000000 | bytes 1000000 | tf_op jit(solution)/shard_map/pallas_call | solution.py:183
  111.9 12.2 %all_to_all.43.own_ref = f32[8,4,16,384]{3,2,1,0:T(8,128)} all-to-all(f32[8,4,16,384]{3,2,1,0:T(8,128)S(1)} %get-tuple-element.22), channel_id=1, replica_groups=mesh['zt'=2,'z1'=2,'z0'=2,'core'=2,'yh'=2,'yl'=2,'x'=4] {'yl','x'}, dimensions={0} | all-to-all | bytes 1572864 | tf_op jit(solution)/shard_map/all_to_all | solution.py:199
  124.2 6.5 %collective-permute-start.1 = (f32[8,4,16,384]{3,2,1,0:T(8,128)}, f32[8,4,16,384]{3,2,1,0:T(8,128)}, u32[]{:S(2)}, u32[]{:S(2)}) collective-permute-start(f32[8,4,16,384]{3,2,1,0:T(8,128)} %all_to_all.43.own_ref), channel_id=1, source_target_pairs={{0,16},{16,0},{1,17},{17,1},{2,18},{18,2},{3,19},{19,3},{4,20},{20... | collective-permute-start | bytes 2359304 | tf_op jit(solution)/shard_map/ppermute | solution.py:195
  130.7 3.5 %all-to-all-start.4 = ((f32[8,9,16,128]{3,2,1,0:T(8,128)}), f32[8,9,16,128]{3,2,1,0:T(8,128)S(1)}, u32[]{:S(2)}, u32[]{:S(2)}) async-start(f32[8,9,16,128]{3,2,1,0:T(8,128)} %copy-done.2), calls=%async_computation.4 | async-start | bytes 1179648 | tf_op jit(solution)/shard_map/all_to_all | solution.py:199
  134.2 5.3 %shard_map.31 = (f32[384,128]{1,0:T(8,128)S(1)}, f32[384,256]{1,0:T(8,128)S(1)}) custom-call(f32[8,4,16,384]{3,2,1,0:T(8,128)} %all_to_all.43.own_ref, f32[8,4,16,384]{3,2,1,0:T(8,128)} %collective-permute-done.1.other_ref), custom_call_target="tpu_custom_call" | custom-call | flops 100000000 | bytes 1000000 | tf_op jit(solution)/shard_map/pallas_call | solution.py:183
  141.0 4.2 %all-to-all-done.4.x01_ref = f32[8,9,16,128]{3,2,1,0:T(8,128)S(1)} async-done(((f32[8,9,16,128]{3,2,1,0:T(8,128)}), f32[8,9,16,128]{3,2,1,0:T(8,128)S(1)}, u32[]{:S(2)}, u32[]{:S(2)}) %all-to-all-start.4) | async-done | bytes 589856 | tf_op jit(solution)/shard_map/all_to_all | solution.py:199
  146.0 2.6 %shard_map.32 = (f32[16,3,8,512]{3,2,1,0:T(8,128)S(1)}, f32[16,2,8,512]{3,2,1,0:T(8,128)S(1)}) custom-call(f32[16,11,8,512]{3,2,1,0:T(8,128)S(1)} %all_to_all.40.a_ref, f32[8,9,16,128]{3,2,1,0:T(8,128)S(1)} %all-to-all-done.4.x01_ref, f32[384,128]{1,0:T(8,128)S(1)} %copy-done.9), custom_call_target="tpu_custom_call" | custom-call | flops 100000000 | bytes 1000000 | tf_op jit(solution)/shard_map/pallas_call | solution.py:183
  150.4 4.5 %all-to-all-start.6 = ((f32[16,3,8,512]{3,2,1,0:T(8,128)}), f32[16,3,8,512]{3,2,1,0:T(8,128)S(1)}, u32[]{:S(2)}, u32[]{:S(2)}) async-start(f32[16,3,8,512]{3,2,1,0:T(8,128)} %copy-done), calls=%async_computation.6 | async-start | bytes 1572864 | tf_op jit(solution)/shard_map/all_to_all | solution.py:199
  154.9 3.8 %collective-permute-start.2 = (f32[384,256]{1,0:T(8,128)}, f32[384,256]{1,0:T(8,128)S(1)}, u32[]{:S(2)}, u32[]{:S(2)}) collective-permute-start(f32[384,256]{1,0:T(8,128)} %copy-done.6), channel_id=1, source_target_pairs={{0,32},{32,0},{1,33},{33,1},{2,34},{34,2},{3,35},{35,3},{4,36},{36... | collective-permute-start | bytes 1179656 | tf_op jit(solution)/shard_map/ppermute | solution.py:195
  158.7 9.0 %collective-permute-done.2.other_ref = f32[384,256]{1,0:T(8,128)S(1)} collective-permute-done((f32[384,256]{1,0:T(8,128)}, f32[384,256]{1,0:T(8,128)S(1)}, u32[]{:S(2)}, u32[]{:S(2)}) %collective-permute-start.2) | collective-permute-done | bytes 393248 | tf_op jit(solution)/shard_map/ppermute | solution.py:195
  168.6 3.1 %shard_map.33 = (f32[256,128]{1,0:T(8,128)S(1)}, f32[256,128]{1,0:T(8,128)S(1)}) custom-call(f32[384,256]{1,0:T(8,128)S(1)} %copy-done.7, f32[384,256]{1,0:T(8,128)S(1)} %collective-permute-done.2.other_ref), custom_call_target="tpu_custom_call" | custom-call | flops 100000000 | bytes 1000000 | tf_op jit(solution)/shard_map/pallas_call | solution.py:183
  171.7 3.4 %collective-permute-start.3 = (f32[256,128]{1,0:T(8,128)S(1)}, f32[256,128]{1,0:T(8,128)S(1)}, u32[]{:S(2)}, u32[]{:S(2)}) collective-permute-start(f32[256,128]{1,0:T(8,128)S(1)} %get-tuple-element.28.own_ref), channel_id=1, source_target_pairs={{0,64},{64,0},{1,65},{65,1},{2,66},{66,2},{3,67},{67,3},{4,68},{68... | collective-permute-start | bytes 393224 | tf_op jit(solution)/shard_map/ppermute | solution.py:195
  175.7 5.3 %collective-permute-done.3.other_ref = f32[256,128]{1,0:T(8,128)S(1)} collective-permute-done((f32[256,128]{1,0:T(8,128)S(1)}, f32[256,128]{1,0:T(8,128)S(1)}, u32[]{:S(2)}, u32[]{:S(2)}) %collective-permute-start.3) | collective-permute-done | bytes 131104 | tf_op jit(solution)/shard_map/ppermute | solution.py:195
  181.0 2.3 %shard_map.35.x4_ref = f32[128,128]{1,0:T(8,128)S(1)} custom-call(f32[256,128]{1,0:T(8,128)S(1)} %get-tuple-element.28.own_ref, f32[256,128]{1,0:T(8,128)S(1)} %collective-permute-done.3.other_ref), custom_call_target="tpu_custom_call" | custom-call | flops 100000000 | bytes 1000000 | tf_op jit(solution)/shard_map/pallas_call | solution.py:183
  183.7 16.2 %all_to_all.44 = f32[16,2,8,512]{3,2,1,0:T(8,128)S(1)} all-to-all(f32[16,2,8,512]{3,2,1,0:T(8,128)S(1)} %shard_map.36), channel_id=1, replica_groups=mesh['zt'=2,'z1'=2,'z0'=2,'core'=2,'yh'=2,'yl'=2,'x'=4] {'yh','yl','x'}, dimensions={0} | all-to-all | bytes 1048576 | tf_op jit(solution)/shard_map/all_to_all | solution.py:199
  (35 shorter events, 12.1 us)
Async XLA Ops:
  93.6 0.8 copy-start.3
  94.4 0.6 copy-start.10
  95.0 12.9 %all-to-all-start.3 = ((f32[16,16,512]{2,1,0:T(8,128)}), f32[16,16,512]{2,1,0:T(8,128)S(1)}, u32[]{:S(2)}, u32[]{:S(2)}) async-start(f32[16,16,512]{2,1,0:T(8,128)} %copy-done.3), calls=%async_computation.3 | async-start | bytes 1048576 | tf_op jit(solution)/shard_map/all_to_all | solution.py:199
  98.6 7.0 %collective-permute-start = (f32[4,16,512]{2,1,0:T(8,128)S(1)}, f32[4,16,512]{2,1,0:T(8,128)}, u32[]{:S(2)}, u32[]{:S(2)}) collective-permute-start(f32[4,16,512]{2,1,0:T(8,128)S(1)} %get-tuple-element.19.own_ref), channel_id=1, source_target_pairs={{0,8},{8,0},{1,9},{9,1},{2,10},{10,2},{3,11},{11,3},{4,12},{12,4},... | collective-permute-start | bytes 393224 | tf_op jit(solution)/shard_map/ppermute | solution.py:195
  107.9 0.9 copy-start.11
  111.9 18.7 %copy-start.2 = (f32[8,9,16,128]{3,2,1,0:T(8,128)}, f32[8,9,16,128]{3,2,1,0:T(8,128)S(1)}, u32[]{:S(2)}) copy-start(f32[8,9,16,128]{3,2,1,0:T(8,128)S(1)} %get-tuple-element.21) | copy-start | bytes 1769476
  124.2 10.1 %collective-permute-start.1 = (f32[8,4,16,384]{3,2,1,0:T(8,128)}, f32[8,4,16,384]{3,2,1,0:T(8,128)}, u32[]{:S(2)}, u32[]{:S(2)}) collective-permute-start(f32[8,4,16,384]{3,2,1,0:T(8,128)} %all_to_all.43.own_ref), channel_id=1, source_target_pairs={{0,16},{16,0},{1,17},{17,1},{2,18},{18,2},{3,19},{19,3},{4,20},{20... | collective-permute-start | bytes 2359304 | tf_op jit(solution)/shard_map/ppermute | solution.py:195
  130.7 14.4 %all-to-all-start.4 = ((f32[8,9,16,128]{3,2,1,0:T(8,128)}), f32[8,9,16,128]{3,2,1,0:T(8,128)S(1)}, u32[]{:S(2)}, u32[]{:S(2)}) async-start(f32[8,9,16,128]{3,2,1,0:T(8,128)} %copy-done.2), calls=%async_computation.4 | async-start | bytes 1179648 | tf_op jit(solution)/shard_map/all_to_all | solution.py:199
  139.5 0.8 copy-start.6
  140.3 0.7 copy-start.8
  145.1 0.9 copy-start.9
  148.7 0.9 copy-start
  149.6 0.8 copy-start.4
  150.4 24.7 %copy-start.1 = (f32[16,3,8,512]{3,2,1,0:T(8,128)S(1)}, f32[16,3,8,512]{3,2,1,0:T(8,128)}, u32[]{:S(2)}) copy-start(f32[16,3,8,512]{3,2,1,0:T(8,128)} %copy-done) | copy-start | bytes 2359300
  150.4 24.7 %copy-start.5 = (f32[16,2,8,512]{3,2,1,0:T(8,128)S(1)}, f32[16,2,8,512]{3,2,1,0:T(8,128)}, u32[]{:S(2)}) copy-start(f32[16,2,8,512]{3,2,1,0:T(8,128)} %copy-done.4) | copy-start | bytes 1572868
  150.4 33.3 %all-to-all-start.6 = ((f32[16,3,8,512]{3,2,1,0:T(8,128)}), f32[16,3,8,512]{3,2,1,0:T(8,128)S(1)}, u32[]{:S(2)}, u32[]{:S(2)}) async-start(f32[16,3,8,512]{3,2,1,0:T(8,128)} %copy-done), calls=%async_computation.6 | async-start | bytes 1572864 | tf_op jit(solution)/shard_map/all_to_all | solution.py:199
  154.9 12.8 %collective-permute-start.2 = (f32[384,256]{1,0:T(8,128)}, f32[384,256]{1,0:T(8,128)S(1)}, u32[]{:S(2)}, u32[]{:S(2)}) collective-permute-start(f32[384,256]{1,0:T(8,128)} %copy-done.6), channel_id=1, source_target_pairs={{0,32},{32,0},{1,33},{33,1},{2,34},{34,2},{3,35},{35,3},{4,36},{36... | collective-permute-start | bytes 1179656 | tf_op jit(solution)/shard_map/ppermute | solution.py:195
  167.6 1.0 copy-start.7
  171.7 9.2 %collective-permute-start.3 = (f32[256,128]{1,0:T(8,128)S(1)}, f32[256,128]{1,0:T(8,128)S(1)}, u32[]{:S(2)}, u32[]{:S(2)}) collective-permute-start(f32[256,128]{1,0:T(8,128)S(1)} %get-tuple-element.28.own_ref), channel_id=1, source_target_pairs={{0,64},{64,0},{1,65},{65,1},{2,66},{66,2},{3,67},{67,3},{4,68},{68... | collective-permute-start | bytes 393224 | tf_op jit(solution)/shard_map/ppermute | solution.py:195
where the time goes:
time: 202 us; the launch traced here: 201 us
  blocking collectives  110 us (54%)
  starting transfers between devices  28.1 us (14%)
  Pallas kernels  26.8 us (13%)
  waiting for transfers between devices  24.9 us (12%)
  local copies, waits for them, and re-layouts  8.87 us (4%)
  other arithmetic  2.24 us (1%)
    all_to_all x5, blocking collectives, spread(): return lax.all_to_all(value, axes, 0, 0, tiled=True)  110 us
    pallas_call x9, Pallas kernels, call(): pl.pallas_call(kernel, out_shape=shapes, in_specs=specs, out_specs=[vmem]...  26.8 us
    ppermute x4, waiting for transfers between devices, exchange(): return lax.ppermute(value, axis, [(0, 1), (1, 0)])  18.4 us
    ppermute x4, starting transfers between devices, exchange(): return lax.ppermute(value, axis, [(0, 1), (1, 0)])  16.5 us
    all_to_all x3, starting transfers between devices, spread(): return lax.all_to_all(value, axes, 0, 0, tiled=True)  11.6 us
    unnamed x24, local copies, waits for them, and re-layouts  7.37 us
    all_to_all x3, waiting for transfers between devices, spread(): return lax.all_to_all(value, axes, 0, 0, tiled=True)  6.47 us
  transfers between devices with their start and end apart: 7, of which 5 were waited for; matrix products, arithmetic and copies ran while one was open for 0% of the time, Pallas kernels for 6%

commit v1 on v0

v1 whole, which is shorter than its diff:
```python
import functools

import jax
import jax.numpy as jnp
import numpy as np
from jax import lax
from jax.experimental import pallas as pl
from jax.experimental.pallas import tpu as pltpu
from jax.sharding import Mesh
from jax.sharding import PartitionSpec as P

ROWS = ("zt", "z1", "z0", "core")
COLS = ("yh", "yl", "x")
GROUP = ("yl", "x")
LEVELS = 6
K = 128
HIGHEST = lax.Precision.HIGHEST


def dot(a, b):
    return jnp.dot(a, b, precision=HIGHEST, preferred_element_type=jnp.float32)


def dot_t(a, b):
    return lax.dot_general(a, b, (((1,), (1,)), ((), ())), precision=HIGHEST, preferred_element_type=jnp.float32)


def inverse(coupling, x_ref, r_ref):
    rows = lax.broadcasted_iota(jnp.int32, (K, K), 0)
    cols = lax.broadcasted_iota(jnp.int32, (K, K), 1)
    eye = jnp.where(rows == cols, 1.0, 0.0).astype(jnp.float32)
    matrix = eye - coupling
    x = eye + coupling
    x = x + dot(dot(coupling, coupling), x)
    r = eye - dot(x, matrix)
    size = jnp.sum(r * r)
    x_ref[...] = x + dot(r, x)

    @pl.when(jnp.logical_not(size < 1e-6))
    def _():
        @pl.when(jnp.logical_not(size < 0.25))
        def _():
            weight = jnp.abs(matrix)
            scale = 1.0 / (jnp.max(jnp.sum(weight, axis=0)) * jnp.max(jnp.sum(weight, axis=1)))
            x_ref[...] = matrix.T * scale

        def residual():
            r = eye - dot(x_ref[...], matrix)
            r_ref[...] = r
            return jnp.sum(r * r)

        def refine():
            x_ref[...] = x_ref[...] + dot(r_ref[...], x_ref[...])

        def going(carry):
            step, size = carry
            return jnp.logical_and(step < 80, size > 1e-6)

        def again(carry):
            step, _ = carry
            refine()
            return step + 1, residual()

        lax.while_loop(going, again, (jnp.int32(0), residual()))
        refine()


def eliminate(panel1, panel2, rest1, rest2, x_ref, r_ref):
    target = rest2[:, :K] - dot(rest1[:, :K], panel2[:, :K])
    inverse(dot(panel1[:, :K], panel2[:, :K]), x_ref, r_ref)
    return substitute(panel1, panel2, rest1, rest2, target, x_ref)


def substitute(panel1, panel2, rest1, rest2, target, x_ref):
    x1 = dot(target, x_ref[...])
    x2 = rest1[:, :K] - dot(x1, panel1[:, :K])
    if panel1.shape[1] == K:
        return x1, x2, None
    state = rest1[:, K:] + rest2[:, K:] - dot(x1, panel1[:, K:]) - dot(x2, panel2[:, K:])
    return x1, x2, state


def unpack_kernel(early_ref, late_ref, o_ref):
    for part in range(16):
        cut = slice(part * 512, (part + 1) * 512)
        o_ref[:3, :, cut] = early_ref[part]
        o_ref[3:, :, cut] = late_ref[part]


def gram_kernel(steps, ids_ref, a_ref, *g_refs):
    right = a_ref[:, LEVELS:]
    right = jnp.transpose(right, (1, 0, 2, 3)).reshape((LEVELS - 1) * K, -1)
    left = []
    for step in steps:
        member = jnp.bitwise_xor(ids_ref[0], step)
        block = a_ref[pl.ds(2 * member, 2), :LEVELS]
        left.append(jnp.transpose(block, (1, 0, 2, 3)).reshape(LEVELS * 16, -1))
    gram = dot_t(jnp.concatenate(left, axis=0), right)
    for at, g_ref in enumerate(g_refs):
        g_ref[...] = gram[at * LEVELS * 16 : (at + 1) * LEVELS * 16].reshape(LEVELS, 16, -1)


def level0_kernel(ids_ref, ag_ref, own_ref, other_ref, x_out, panel_out, rest_out, x_ref, r_ref):
    width = (LEVELS - 1) * K
    side = ids_ref[1]

    def panel(at):
        return jnp.concatenate([ag_ref[:4, at], ag_ref[4:, 1 - at]], axis=0).reshape(K, width)

    n = LEVELS - 1
    x1, x2, state = eliminate(
        panel(side),
        panel(1 - side),
        own_ref[1:].reshape(n * 16, width),
        other_ref[1:].reshape(n * 16, width),
        x_ref,
        r_ref,
    )
    state = state.reshape(n, 16, width - K)
    panel_out[...] = jnp.broadcast_to(state[0], panel_out.shape)
    rest_out[...] = state[1:]
    x_out[side] = x1.reshape(n, 16, K)
    x_out[1 - side] = x2.reshape(n, 16, K)


def level1_panels(ids_ref, ag_ref):
    width = (LEVELS - 2) * K
    side = ids_ref[2]
    p1 = ag_ref[pl.ds(side * 8, 8)].reshape(K, width)
    p2 = ag_ref[pl.ds((1 - side) * 8, 8)].reshape(K, width)
    return p1, p2


def level1_inverse_kernel(ids_ref, ag_ref, x_ref, r_ref):
    p1, p2 = level1_panels(ids_ref, ag_ref)
    inverse(dot(p1[:, :K], p2[:, :K]), x_ref, r_ref)


def level1_kernel(ids_ref, ag_ref, own_ref, other_ref, x0_ref, inverse_ref, x_out, s_out):
    width = (LEVELS - 2) * K
    n = LEVELS - 2
    p1, p2 = level1_panels(ids_ref, ag_ref)
    own, other = own_ref[...].reshape(n * 16, width), other_ref[...].reshape(n * 16, width)
    target = other[:, :K] - dot(own[:, :K], p2[:, :K])
    x1, _, state = substitute(p1, p2, own, other, target, inverse_ref)
    half = (4, n + 1, 16, K)
    x_out[:4, : n + 1] = jnp.broadcast_to(x0_ref[0], half)
    x_out[4:, : n + 1] = jnp.broadcast_to(x0_ref[1], half)
    x_out[:, n + 1 :] = jnp.broadcast_to(x1.reshape(n, 16, K), (8, n, 16, K))
    s_out[...] = jnp.broadcast_to(state.reshape(n, 16, width - K), s_out.shape)


def level2_kernel(own_ref, other_ref, x_out, s_out, x_ref, r_ref):
    width = (LEVELS - 3) * K
    n = LEVELS - 3

    def rest(ref):
        return jnp.concatenate([ref[:, m].reshape(K, width) for m in range(1, n + 1)], axis=0)

    x1, _, state = eliminate(
        own_ref[:, 0].reshape(K, width), other_ref[:, 0].reshape(K, width), rest(own_ref), rest(other_ref), x_ref, r_ref
    )
    x_out[...] = x1
    s_out[...] = state


def level3_kernel(own_ref, other_ref, x_out, s_out, x_ref, r_ref):
    x1, _, state = eliminate(own_ref[:K], other_ref[:K], own_ref[K:], other_ref[K:], x_ref, r_ref)
    x_out[...] = x1
    s_out[...] = state


def level4_kernel(own_ref, other_ref, x_out, x_ref, r_ref):
    x1, _, _ = eliminate(own_ref[:K], other_ref[:K], own_ref[K:], other_ref[K:], x_ref, r_ref)
    x_out[...] = x1


def finish_kernel(a_ref, x01_ref, x2_ref, o_ref, part_ref):
    done = [a_ref[:, 0].reshape(K, -1)]

    def factor(level, i):
        if level == 2:
            return x2_ref[i * K : (i + 1) * K]
        return x01_ref[:, (LEVELS - 1) * level + i].reshape(K, K)

    for m in range(1, LEVELS):
        value = a_ref[:, m].reshape(K, -1)
        for level in range(min(m, 3)):
            value = value - dot(factor(level, m - level - 1), done[level])
        done.append(value)
        if m < 4:
            o_ref[:, m - 1] = value.reshape(16, 8, -1)
        else:
            part_ref[:, m - 4] = value.reshape(16, 8, -1)


def later_kernel(o_ref, part_ref, x3_ref, r_ref):
    base = o_ref[:, 2].reshape(K, -1)
    for i in range(2):
        value = part_ref[:, i].reshape(K, -1) - dot(x3_ref[i * K : (i + 1) * K], base)
        r_ref[:, i] = value.reshape(16, 8, -1)


def last_kernel(part_ref, x4_ref, r_ref):
    base = part_ref[:, 0]
    value = part_ref[:, 1].reshape(K, -1) - dot(x4_ref[...], base.reshape(K, -1))
    r_ref[:, 0] = base
    r_ref[:, 1] = value.reshape(16, 8, -1)


def call(kernel, outs, *args, scalar=False, flops=10**8, name=None):
    name = name or kernel.__name__
    vmem = pl.BlockSpec(memory_space=pltpu.VMEM)
    specs = [vmem] * len(args)
    square = pltpu.VMEM((K, K), jnp.float32)
    scratch = []
    if scalar:
        specs[0] = pl.BlockSpec(memory_space=pltpu.SMEM)
    if name == "level1_inverse_kernel":
        scratch = [square]
    elif name.startswith("level") and name != "level1_kernel":
        scratch = [square] * 2
    return pl.pallas_call(
        kernel,
        out_shape=[jax.ShapeDtypeStruct(s, jnp.float32) for s in outs],
        in_specs=specs,
        out_specs=[vmem] * len(outs),
        scratch_shapes=scratch,
        compiler_params=pltpu.CompilerParams(vmem_limit_bytes=LIMIT[name] << 20),
        cost_estimate=pl.CostEstimate(flops=flops, bytes_accessed=10**6, transcendentals=0),
    )(*args)


def exchange(value, axis):
    return lax.ppermute(value, axis, [(0, 1), (1, 0)])


def reach(value, step):
    if step == 0:
        return value
    return lax.ppermute(value, GROUP, [(at, at ^ step) for at in range(8)])


def spread(value, axes):
    return lax.all_to_all(value, axes, 0, 0, tiled=True)


def steps(solved, right):
    ids = jnp.stack([lax.axis_index(GROUP), lax.axis_index("yl"), lax.axis_index("yh")]).astype(jnp.int32)
    solved, ids = lax.optimization_barrier((solved, ids))
    both = jnp.concatenate([solved, right], axis=0)
    packed = both.reshape(both.shape[0], 8, 16, 512).transpose(2, 0, 1, 3)
    rows = spread(packed, COLS)
    shape = (LEVELS, 16, (LEVELS - 1) * K)
    grams = {}
    for name, chosen in (("gram_far_kernel", (5, 6, 7, 4)), ("gram_near_kernel", (2, 1, 3, 0))):
        made = call(functools.partial(gram_kernel, chosen), [shape] * 4, ids, rows, scalar=True, flops=10**9, name=name)
        grams.update({step: reach(g, step) for step, g in zip(chosen, made)})
    own = grams[0] + grams[1] + grams[2] + grams[3]
    other = grams[4] + grams[5] + grams[6] + grams[7]

    slices = jnp.broadcast_to(jnp.stack([own[0], other[0]]), (8, 2, 16, (LEVELS - 1) * K))
    panels = spread(slices, GROUP)
    outs = [(2, 5, 16, K), (16, 16, 4 * K), (4, 16, 4 * K)]
    x0, panel, rest = call(level0_kernel, outs, ids, panels, own, other, scalar=True)

    other = exchange(rest, "yh")
    panels = spread(panel, COLS)
    (inv,) = call(level1_inverse_kernel, [(K, K)], ids, panels, scalar=True)
    outs = [(8, 9, 16, K), (8, 4, 16, 3 * K)]
    x01, s1 = call(level1_kernel, outs, ids, panels, rest, other, x0, inv, scalar=True)

    s1 = spread(s1, GROUP)
    other = exchange(s1, "core")
    x01 = spread(x01, GROUP)
    x2, s2 = call(level2_kernel, [(3 * K, K), (3 * K, 2 * K)], s1, other)
    other = exchange(s2, "z0")
    early, part = call(finish_kernel, [(16, 3, 8, 512), (16, 2, 8, 512)], rows, x01, x2)
    early_out = spread(early, COLS)
    x3, s3 = call(level3_kernel, [(2 * K, K), (2 * K, K)], s2, other)
    other = exchange(s3, "z1")
    (part,) = call(later_kernel, [(16, 2, 8, 512)], early, part, x3)
    (x4,) = call(level4_kernel, [(K, K)], s3, other)
    (late,) = call(last_kernel, [(16, 2, 8, 512)], part, x4)
    late, early_out = lax.optimization_barrier((late, early_out))
    late = spread(late, COLS)
    (out,) = call(unpack_kernel, [(LEVELS - 1, 8, 8192)], early_out, late)
    return out


def solution(mesh):
    fine = Mesh(np.array(mesh.devices).reshape(2, 2, 2, 2, 2, 2, 4), ROWS + COLS)
    spec = P(None, COLS, ROWS)
    return jax.shard_map(steps, mesh=fine, in_specs=(spec, spec), out_specs=spec, check_vma=False)


LIMIT = dict(
    unpack_kernel=12,
    gram_far_kernel=24,
    gram_near_kernel=24,
    level0_kernel=12,
    level1_inverse_kernel=12,
    level1_kernel=12,
    level2_kernel=12,
    level3_kernel=12,
    level4_kernel=12,
    finish_kernel=24,
    later_kernel=12,
    last_kernel=12,
)
```

time: 202 us -> 207 us (1.025)
  waiting for transfers between devices: 24.9 us -> 49.6 us
  blocking collectives: 110 us -> 87.7 us
  starting transfers between devices: 28.1 us -> 31.3 us
    ppermute x0 -> x7, waiting for transfers between devices: none -> 25.3 us  [reach(): return lax.ppermute(value, GROUP, [(at, at ^ step) for at in range(8)])]
    all_to_all x5 -> x4, blocking collectives: 110 us -> 87.7 us  [spread(): return lax.all_to_all(value, axes, 0, 0, tiled=True)]
    ppermute x0 -> x7, starting transfers between devices: none -> 8.8 us  [reach(): return lax.ppermute(value, GROUP, [(at, at ^ step) for at in range(8)])]
    ppermute x4, waiting for transfers between devices: 18.4 us -> 12.1 us  [exchange(): return lax.ppermute(value, axis, [(0, 1), (1, 0)])]
    all_to_all x3, waiting for transfers between devices: 6.47 us -> 12.2 us  [spread(): return lax.all_to_all(value, axes, 0, 0, tiled=True)]
    ppermute x4, starting transfers between devices: 16.5 us -> 11.6 us  [exchange(): return lax.ppermute(value, axis, [(0, 1), (1, 0)])]
    unnamed x24, local copies, waits for them, and re-layouts: 7.37 us -> 9.47 us
    pallas_call x9 -> x12, Pallas kernels: 26.8 us -> 25 us  [call(): pl.pallas_call(kernel, out_shape=[jax.ShapeDtypeStruct(s, jnp.float32) fo...]
  transfers between devices with their start and end apart: 7 -> 14, of which waited for: 5 -> 7; matrix products, arithmetic and copies ran while one was open for 0% -> 0% of each run, Pallas kernels for 6% -> 7%
where the time goes in v1:
time: 207 us; the launch traced here: 206 us
  blocking collectives  87.7 us (42%)
  waiting for transfers between devices  49.6 us (24%)
  starting transfers between devices  31.3 us (15%)
  Pallas kernels  25 us (12%)
  local copies, waits for them, and re-layouts  9.8 us (5%)
  other arithmetic  2.21 us (1%)
    all_to_all x4, blocking collectives, spread(): return lax.all_to_all(value, axes, 0, 0, tiled=True)  87.7 us
    ppermute x7, waiting for transfers between devices, reach(): return lax.ppermute(value, GROUP, [(at, at ^ step) for at in range(8)])  25.3 us
    pallas_call x12, Pallas kernels, call(): pl.pallas_call(kernel, out_shape=[jax.ShapeDtypeStruct(s, jnp.float32) fo...  25 us
    all_to_all x3, waiting for transfers between devices, spread(): return lax.all_to_all(value, axes, 0, 0, tiled=True)  12.2 us
    ppermute x4, waiting for transfers between devices, exchange(): return lax.ppermute(value, axis, [(0, 1), (1, 0)])  12.1 us
    ppermute x4, starting transfers between devices, exchange(): return lax.ppermute(value, axis, [(0, 1), (1, 0)])  11.6 us
    all_to_all x3, starting transfers between devices, spread(): return lax.all_to_all(value, axes, 0, 0, tiled=True)  10.9 us
    unnamed x24, local copies, waits for them, and re-layouts  9.47 us
  transfers between devices with their start and end apart: 14, of which 7 were waited for; matrix products, arithmetic and copies ran while one was open for 0% of the time, Pallas kernels for 7%

profile of v1, /device:TPU:1, one launch (start us, length us, event | category | flops | bytes accessed | tf_op | source)
XLA Modules:
  0.0 205.9 jit_solution(17436081035675658275)
XLA Ops:
  2.4 43.4 %all_to_all.35.a_ref = f32[16,11,8,512]{3,2,1,0:T(8,128)S(1)} all-to-all(f32[16,11,8,512]{3,2,1,0:T(8,128)S(1)} %bitcast.10), channel_id=1, replica_groups=mesh['zt'=2,'z1'=2,'z0'=2,'core'=2,'yh'=2,'yl'=2,'x'=4] {'yh','yl','x'}, dimensions={0} | all-to-all | bytes 5767168 | tf_op jit(solution)/shard_map/all_to_all | solution.py:245
  45.8 2.6 %shard_map.29 = (f32[6,16,640]{2,1,0:T(8,128)S(1)}, f32[6,16,640]{2,1,0:T(8,128)S(1)}, f32[6,16,640]{2,1,0:T(8,128)S(1)}, f32[6,16,640]{2,1,0:T(8,128)S(1)}) custom-call(s32[3]{0:T(128)S(1)} %pad_add_fusion.ids_ref, f32[16,11,8,512]{3,2,1,0:T(8,128)S(1)} %all_to_all.35.a_ref), custom_call_target="tpu_custom_call" | custom-call | flops 1000000000 | bytes 1000000 | tf_op jit(solution)/shard_map/pallas_call | solution.py:223
  51.2 3.2 %collective-permute-start.6 = (f32[6,16,640]{2,1,0:T(8,128)S(1)}, f32[6,16,640]{2,1,0:T(8,128)S(1)}, u32[]{:S(2)}, u32[]{:S(2)}) collective-permute-start(f32[6,16,640]{2,1,0:T(8,128)S(1)} %get-tuple-element.37), channel_id=1, source_target_pairs={{0,7},{1,6},{2,5},{3,4},{4,3},{5,2},{6,1},{7,0},{8,15},{9,14},{10,... | collective-permute-start | bytes 737288 | tf_op jit(solution)/shard_map/ppermute | solution.py:241
  54.4 2.6 %shard_map.28 = (f32[6,16,640]{2,1,0:T(8,128)S(1)}, f32[6,16,640]{2,1,0:T(8,128)S(1)}, f32[6,16,640]{2,1,0:T(8,128)S(1)}, f32[6,16,640]{2,1,0:T(8,128)S(1)}) custom-call(s32[3]{0:T(128)S(1)} %pad_add_fusion.ids_ref, f32[16,11,8,512]{3,2,1,0:T(8,128)S(1)} %all_to_all.35.a_ref), custom_call_target="tpu_custom_call" | custom-call | flops 1000000000 | bytes 1000000 | tf_op jit(solution)/shard_map/pallas_call | solution.py:223
  57.2 14.0 %collective-permute-done.3 = f32[6,16,640]{2,1,0:T(8,128)S(1)} collective-permute-done((f32[6,16,640]{2,1,0:T(8,128)S(1)}, f32[6,16,640]{2,1,0:T(8,128)S(1)}, u32[]{:S(2)}, u32[]{:S(2)}) %collective-permute-start.3) | collective-permute-done | bytes 245792 | tf_op jit(solution)/shard_map/ppermute | solution.py:241
  71.2 2.7 %collective-permute-start.2 = (f32[6,16,640]{2,1,0:T(8,128)S(1)}, f32[6,16,640]{2,1,0:T(8,128)S(1)}, u32[]{:S(2)}, u32[]{:S(2)}) collective-permute-start(f32[6,16,640]{2,1,0:T(8,128)S(1)} %get-tuple-element.33), channel_id=1, source_target_pairs={{0,3},{1,2},{2,1},{3,0},{4,7},{5,6},{6,5},{7,4},{8,11},{9,10},{10,... | collective-permute-start | bytes 737288 | tf_op jit(solution)/shard_map/ppermute | solution.py:241
  73.9 4.8 %collective-permute-done.1 = f32[6,16,640]{2,1,0:T(8,128)S(1)} collective-permute-done((f32[6,16,640]{2,1,0:T(8,128)S(1)}, f32[6,16,640]{2,1,0:T(8,128)S(1)}, u32[]{:S(2)}, u32[]{:S(2)}) %collective-permute-start.1) | collective-permute-done | bytes 245792 | tf_op jit(solution)/shard_map/ppermute | solution.py:241
  78.8 6.5 %collective-permute-done.2 = f32[6,16,640]{2,1,0:T(8,128)S(1)} collective-permute-done((f32[6,16,640]{2,1,0:T(8,128)S(1)}, f32[6,16,640]{2,1,0:T(8,128)S(1)}, u32[]{:S(2)}, u32[]{:S(2)}) %collective-permute-start.2) | collective-permute-done | bytes 245792 | tf_op jit(solution)/shard_map/ppermute | solution.py:241
  85.4 13.6 %all_to_all.36.ag_ref = f32[8,2,16,640]{3,2,1,0:T(8,128)S(1)} all-to-all(f32[8,2,16,640]{3,2,1,0:T(8,128)S(1)} %broadcast_in_dim.3), channel_id=1, replica_groups=mesh['zt'=2,'z1'=2,'z0'=2,'core'=2,'yh'=2,'yl'=2,'x'=4] {'yl','x'}, dimensions={0} | all-to-all | bytes 1310720 | tf_op jit(solution)/shard_map/all_to_all | solution.py:245
  102.8 3.6 %all-to-all-start.2 = ((f32[16,16,512]{2,1,0:T(8,128)}), f32[16,16,512]{2,1,0:T(8,128)S(1)}, u32[]{:S(2)}, u32[]{:S(2)}) async-start(f32[16,16,512]{2,1,0:T(8,128)} %copy-done.3), calls=%async_computation.2 | async-start | bytes 1048576 | tf_op jit(solution)/shard_map/all_to_all | solution.py:245
  106.4 2.8 %collective-permute-start.7 = (f32[4,16,512]{2,1,0:T(8,128)S(1)}, f32[4,16,512]{2,1,0:T(8,128)}, u32[]{:S(2)}, u32[]{:S(2)}) collective-permute-start(f32[4,16,512]{2,1,0:T(8,128)S(1)} %get-tuple-element.39.own_ref), channel_id=1, source_target_pairs={{0,8},{8,0},{1,9},{9,1},{2,10},{10,2},{3,11},{11,3},{4,12},{12,4},... | collective-permute-start | bytes 393224 | tf_op jit(solution)/shard_map/ppermute | solution.py:235
  109.2 7.3 %all-to-all-done.2.ag_ref = f32[16,16,512]{2,1,0:T(8,128)S(1)} async-done(((f32[16,16,512]{2,1,0:T(8,128)}), f32[16,16,512]{2,1,0:T(8,128)S(1)}, u32[]{:S(2)}, u32[]{:S(2)}) %all-to-all-start.2) | async-done | bytes 524320 | tf_op jit(solution)/shard_map/all_to_all | solution.py:245
  121.0 14.6 %all_to_all.37.own_ref = f32[8,4,16,384]{3,2,1,0:T(8,128)} all-to-all(f32[8,4,16,384]{3,2,1,0:T(8,128)S(1)} %get-tuple-element.42), channel_id=1, replica_groups=mesh['zt'=2,'z1'=2,'z0'=2,'core'=2,'yh'=2,'yl'=2,'x'=4] {'yl','x'}, dimensions={0} | all-to-all | bytes 1572864 | tf_op jit(solution)/shard_map/all_to_all | solution.py:245
  135.6 3.2 %collective-permute-start.8 = (f32[8,4,16,384]{3,2,1,0:T(8,128)}, f32[8,4,16,384]{3,2,1,0:T(8,128)}, u32[]{:S(2)}, u32[]{:S(2)}) collective-permute-start(f32[8,4,16,384]{3,2,1,0:T(8,128)} %all_to_all.37.own_ref), channel_id=1, source_target_pairs={{0,16},{16,0},{1,17},{17,1},{2,18},{18,2},{3,19},{19,3},{4,20},{20... | collective-permute-start | bytes 2359304 | tf_op jit(solution)/shard_map/ppermute | solution.py:235
  138.9 3.5 %all-to-all-start.3 = ((f32[8,9,16,128]{3,2,1,0:T(8,128)}), f32[8,9,16,128]{3,2,1,0:T(8,128)S(1)}, u32[]{:S(2)}, u32[]{:S(2)}) async-start(f32[8,9,16,128]{3,2,1,0:T(8,128)} %copy-done.2), calls=%async_computation.3 | async-start | bytes 1179648 | tf_op jit(solution)/shard_map/all_to_all | solution.py:245
  142.4 4.6 %shard_map.33 = (f32[384,128]{1,0:T(8,128)S(1)}, f32[384,256]{1,0:T(8,128)S(1)}) custom-call(f32[8,4,16,384]{3,2,1,0:T(8,128)} %all_to_all.37.own_ref, f32[8,4,16,384]{3,2,1,0:T(8,128)} %collective-permute-done.8.other_ref), custom_call_target="tpu_custom_call" | custom-call | flops 100000000 | bytes 1000000 | tf_op jit(solution)/shard_map/pallas_call | solution.py:223
  148.4 4.9 %all-to-all-done.3.x01_ref = f32[8,9,16,128]{3,2,1,0:T(8,128)S(1)} async-done(((f32[8,9,16,128]{3,2,1,0:T(8,128)}), f32[8,9,16,128]{3,2,1,0:T(8,128)S(1)}, u32[]{:S(2)}, u32[]{:S(2)}) %all-to-all-start.3) | async-done | bytes 589856 | tf_op jit(solution)/shard_map/all_to_all | solution.py:245
  154.2 2.6 %shard_map.34 = (f32[16,3,8,512]{3,2,1,0:T(8,128)S(1)}, f32[16,2,8,512]{3,2,1,0:T(8,128)S(1)}) custom-call(f32[16,11,8,512]{3,2,1,0:T(8,128)S(1)} %all_to_all.35.a_ref, f32[8,9,16,128]{3,2,1,0:T(8,128)S(1)} %all-to-all-done.3.x01_ref, f32[384,128]{1,0:T(8,128)S(1)} %copy-done.9), custom_call_target="tpu_custom_call" | custom-call | flops 100000000 | bytes 1000000 | tf_op jit(solution)/shard_map/pallas_call | solution.py:223
  158.5 3.8 %all-to-all-start.5 = ((f32[16,3,8,512]{3,2,1,0:T(8,128)}), f32[16,3,8,512]{3,2,1,0:T(8,128)S(1)}, u32[]{:S(2)}, u32[]{:S(2)}) async-start(f32[16,3,8,512]{3,2,1,0:T(8,128)} %copy-done), calls=%async_computation.5 | async-start | bytes 1572864 | tf_op jit(solution)/shard_map/all_to_all | solution.py:245
  164.7 9.0 %collective-permute-done.9.other_ref = f32[384,256]{1,0:T(8,128)S(1)} collective-permute-done((f32[384,256]{1,0:T(8,128)}, f32[384,256]{1,0:T(8,128)S(1)}, u32[]{:S(2)}, u32[]{:S(2)}) %collective-permute-start.9) | collective-permute-done | bytes 393248 | tf_op jit(solution)/shard_map/ppermute | solution.py:235
  174.7 2.6 %shard_map.35 = (f32[256,128]{1,0:T(8,128)S(1)}, f32[256,128]{1,0:T(8,128)S(1)}) custom-call(f32[384,256]{1,0:T(8,128)S(1)} %copy-done.7, f32[384,256]{1,0:T(8,128)S(1)} %collective-permute-done.9.other_ref), custom_call_target="tpu_custom_call" | custom-call | flops 100000000 | bytes 1000000 | tf_op jit(solution)/shard_map/pallas_call | solution.py:223
  177.3 3.1 %collective-permute-start.10 = (f32[256,128]{1,0:T(8,128)S(1)}, f32[256,128]{1,0:T(8,128)S(1)}, u32[]{:S(2)}, u32[]{:S(2)}) collective-permute-start(f32[256,128]{1,0:T(8,128)S(1)} %get-tuple-element.48.own_ref), channel_id=1, source_target_pairs={{0,64},{64,0},{1,65},{65,1},{2,66},{66,2},{3,67},{67,3},{4,68},{68... | collective-permute-start | bytes 393224 | tf_op jit(solution)/shard_map/ppermute | solution.py:235
  183.2 3.1 %collective-permute-done.10.other_ref = f32[256,128]{1,0:T(8,128)S(1)} collective-permute-done((f32[256,128]{1,0:T(8,128)S(1)}, f32[256,128]{1,0:T(8,128)S(1)}, u32[]{:S(2)}, u32[]{:S(2)}) %collective-permute-start.10) | collective-permute-done | bytes 131104 | tf_op jit(solution)/shard_map/ppermute | solution.py:235
  188.6 16.2 %all_to_all.38.late_ref = f32[16,2,8,512]{3,2,1,0:T(8,128)S(1)} all-to-all(f32[16,2,8,512]{3,2,1,0:T(8,128)S(1)} %shard_map.38), channel_id=1, replica_groups=mesh['zt'=2,'z1'=2,'z0'=2,'core'=2,'yh'=2,'yl'=2,'x'=4] {'yh','yl','x'}, dimensions={0} | all-to-all | bytes 1048576 | tf_op jit(solution)/shard_map/all_to_all | solution.py:245
  (53 shorter events, 27.2 us)
Async XLA Ops:
  48.4 22.8 %collective-permute-start.3 = (f32[6,16,640]{2,1,0:T(8,128)S(1)}, f32[6,16,640]{2,1,0:T(8,128)S(1)}, u32[]{:S(2)}, u32[]{:S(2)}) collective-permute-start(f32[6,16,640]{2,1,0:T(8,128)S(1)} %get-tuple-element.34), channel_id=1, source_target_pairs={{0,4},{1,5},{2,6},{3,7},{4,0},{5,1},{6,2},{7,3},{8,12},{9,13},{10,... | collective-permute-start | bytes 737288 | tf_op jit(solution)/shard_map/ppermute | solution.py:241
  48.5 22.7 %collective-permute-start.4 = (f32[6,16,640]{2,1,0:T(8,128)S(1)}, f32[6,16,640]{2,1,0:T(8,128)S(1)}, u32[]{:S(2)}, u32[]{:S(2)}) collective-permute-start(f32[6,16,640]{2,1,0:T(8,128)S(1)} %get-tuple-element.35), channel_id=1, source_target_pairs={{0,5},{1,4},{2,7},{3,6},{4,1},{5,0},{6,3},{7,2},{8,13},{9,12},{10,... | collective-permute-start | bytes 737288 | tf_op jit(solution)/shard_map/ppermute | solution.py:241
  50.0 23.9 %collective-permute-start.5 = (f32[6,16,640]{2,1,0:T(8,128)S(1)}, f32[6,16,640]{2,1,0:T(8,128)S(1)}, u32[]{:S(2)}, u32[]{:S(2)}) collective-permute-start(f32[6,16,640]{2,1,0:T(8,128)S(1)} %get-tuple-element.36), channel_id=1, source_target_pairs={{0,6},{1,7},{2,4},{3,5},{4,2},{5,3},{6,0},{7,1},{8,14},{9,15},{10,... | collective-permute-start | bytes 737288 | tf_op jit(solution)/shard_map/ppermute | solution.py:241
  51.2 22.6 %collective-permute-start.6 = (f32[6,16,640]{2,1,0:T(8,128)S(1)}, f32[6,16,640]{2,1,0:T(8,128)S(1)}, u32[]{:S(2)}, u32[]{:S(2)}) collective-permute-start(f32[6,16,640]{2,1,0:T(8,128)S(1)} %get-tuple-element.37), channel_id=1, source_target_pairs={{0,7},{1,6},{2,5},{3,4},{4,3},{5,2},{6,1},{7,0},{8,15},{9,14},{10,... | collective-permute-start | bytes 737288 | tf_op jit(solution)/shard_map/ppermute | solution.py:241
  57.1 16.8 %collective-permute-start = (f32[6,16,640]{2,1,0:T(8,128)S(1)}, f32[6,16,640]{2,1,0:T(8,128)S(1)}, u32[]{:S(2)}, u32[]{:S(2)}) collective-permute-start(f32[6,16,640]{2,1,0:T(8,128)S(1)} %get-tuple-element.31), channel_id=1, source_target_pairs={{0,1},{1,0},{2,3},{3,2},{4,5},{5,4},{6,7},{7,6},{8,9},{9,8},{10,11... | collective-permute-start | bytes 737288 | tf_op jit(solution)/shard_map/ppermute | solution.py:241
  71.2 7.6 %collective-permute-start.1 = (f32[6,16,640]{2,1,0:T(8,128)S(1)}, f32[6,16,640]{2,1,0:T(8,128)S(1)}, u32[]{:S(2)}, u32[]{:S(2)}) collective-permute-start(f32[6,16,640]{2,1,0:T(8,128)S(1)} %get-tuple-element.32), channel_id=1, source_target_pairs={{0,2},{1,3},{2,0},{3,1},{4,6},{5,7},{6,4},{7,5},{8,10},{9,11},{10,... | collective-permute-start | bytes 737288 | tf_op jit(solution)/shard_map/ppermute | solution.py:241
  71.2 14.1 %collective-permute-start.2 = (f32[6,16,640]{2,1,0:T(8,128)S(1)}, f32[6,16,640]{2,1,0:T(8,128)S(1)}, u32[]{:S(2)}, u32[]{:S(2)}) collective-permute-start(f32[6,16,640]{2,1,0:T(8,128)S(1)} %get-tuple-element.33), channel_id=1, source_target_pairs={{0,3},{1,2},{2,1},{3,0},{4,7},{5,6},{6,5},{7,4},{8,11},{9,10},{10,... | collective-permute-start | bytes 737288 | tf_op jit(solution)/shard_map/ppermute | solution.py:241
  101.4 0.8 copy-start.3
  102.8 13.7 %all-to-all-start.2 = ((f32[16,16,512]{2,1,0:T(8,128)}), f32[16,16,512]{2,1,0:T(8,128)S(1)}, u32[]{:S(2)}, u32[]{:S(2)}) async-start(f32[16,16,512]{2,1,0:T(8,128)} %copy-done.3), calls=%async_computation.2 | async-start | bytes 1048576 | tf_op jit(solution)/shard_map/all_to_all | solution.py:245
  106.4 11.9 %collective-permute-start.7 = (f32[4,16,512]{2,1,0:T(8,128)S(1)}, f32[4,16,512]{2,1,0:T(8,128)}, u32[]{:S(2)}, u32[]{:S(2)}) collective-permute-start(f32[4,16,512]{2,1,0:T(8,128)S(1)} %get-tuple-element.39.own_ref), channel_id=1, source_target_pairs={{0,8},{8,0},{1,9},{9,1},{2,10},{10,2},{3,11},{11,3},{4,12},{12,4},... | collective-permute-start | bytes 393224 | tf_op jit(solution)/shard_map/ppermute | solution.py:235
  118.3 0.9 copy-start.11
  121.0 17.9 %copy-start.2 = (f32[8,9,16,128]{3,2,1,0:T(8,128)}, f32[8,9,16,128]{3,2,1,0:T(8,128)S(1)}, u32[]{:S(2)}) copy-start(f32[8,9,16,128]{3,2,1,0:T(8,128)S(1)} %get-tuple-element.41) | copy-start | bytes 1769476
  135.6 6.8 %collective-permute-start.8 = (f32[8,4,16,384]{3,2,1,0:T(8,128)}, f32[8,4,16,384]{3,2,1,0:T(8,128)}, u32[]{:S(2)}, u32[]{:S(2)}) collective-permute-start(f32[8,4,16,384]{3,2,1,0:T(8,128)} %all_to_all.37.own_ref), channel_id=1, source_target_pairs={{0,16},{16,0},{1,17},{17,1},{2,18},{18,2},{3,19},{19,3},{4,20},{20... | collective-permute-start | bytes 2359304 | tf_op jit(solution)/shard_map/ppermute | solution.py:235
  138.9 14.4 %all-to-all-start.3 = ((f32[8,9,16,128]{3,2,1,0:T(8,128)}), f32[8,9,16,128]{3,2,1,0:T(8,128)S(1)}, u32[]{:S(2)}, u32[]{:S(2)}) async-start(f32[8,9,16,128]{3,2,1,0:T(8,128)} %copy-done.2), calls=%async_computation.3 | async-start | bytes 1179648 | tf_op jit(solution)/shard_map/all_to_all | solution.py:245
  147.0 0.8 copy-start.6
  153.3 0.9 copy-start.9
  156.9 0.9 copy-start
  157.7 0.8 copy-start.4
  158.5 30.0 %all-to-all-start.5 = ((f32[16,3,8,512]{3,2,1,0:T(8,128)}), f32[16,3,8,512]{3,2,1,0:T(8,128)S(1)}, u32[]{:S(2)}, u32[]{:S(2)}) async-start(f32[16,3,8,512]{3,2,1,0:T(8,128)} %copy-done), calls=%async_computation.5 | async-start | bytes 1572864 | tf_op jit(solution)/shard_map/all_to_all | solution.py:245
  162.3 11.4 %collective-permute-start.9 = (f32[384,256]{1,0:T(8,128)}, f32[384,256]{1,0:T(8,128)S(1)}, u32[]{:S(2)}, u32[]{:S(2)}) collective-permute-start(f32[384,256]{1,0:T(8,128)} %copy-done.6), channel_id=1, source_target_pairs={{0,32},{32,0},{1,33},{33,1},{2,34},{34,2},{3,35},{35,3},{4,36},{36... | collective-permute-start | bytes 1179656 | tf_op jit(solution)/shard_map/ppermute | solution.py:235
  173.7 1.0 copy-start.7
  177.3 9.0 %collective-permute-start.10 = (f32[256,128]{1,0:T(8,128)S(1)}, f32[256,128]{1,0:T(8,128)S(1)}, u32[]{:S(2)}, u32[]{:S(2)}) collective-permute-start(f32[256,128]{1,0:T(8,128)S(1)} %get-tuple-element.48.own_ref), channel_id=1, source_target_pairs={{0,64},{64,0},{1,65},{65,1},{2,66},{66,2},{3,67},{67,3},{4,68},{68... | collective-permute-start | bytes 393224 | tf_op jit(solution)/shard_map/ppermute | solution.py:235
  180.5 1.1 copy-start.1
  181.6 1.0 copy-start.5
  (2 other events, 1.3 us)

commit v2 on v1

--- a/solution.py
+++ b/solution.py
@@ -253,8 +253,8 @@
     rows = spread(packed, COLS)
     shape = (LEVELS, 16, (LEVELS - 1) * K)
     grams = {}
-    for name, chosen in (("gram_far_kernel", (5, 6, 7, 4)), ("gram_near_kernel", (2, 1, 3, 0))):
-        made = call(functools.partial(gram_kernel, chosen), [shape] * 4, ids, rows, scalar=True, flops=10**9, name=name)
+    for name, chosen in (("gram_first_kernel", (6, 5)), ("gram_far_kernel", (7, 4)), ("gram_near_kernel", (2, 1, 3, 0))):
+        made = call(functools.partial(gram_kernel, chosen), [shape] * len(chosen), ids, rows, scalar=True, flops=10**9, name=name)
         grams.update({step: reach(g, step) for step, g in zip(chosen, made)})
     own = grams[0] + grams[1] + grams[2] + grams[3]
     other = grams[4] + grams[5] + grams[6] + grams[7]
@@ -296,6 +296,7 @@
 
 LIMIT = dict(
     unpack_kernel=12,
+    gram_first_kernel=24,
     gram_far_kernel=24,
     gram_near_kernel=24,
     level0_kernel=12,
@@ -304,7 +305,7 @@
     level2_kernel=12,
     level3_kernel=12,
     level4_kernel=12,
-    finish_kernel=24,
+    finish_kernel=58,
     later_kernel=12,
     last_kernel=12,
 )

time: 207 us -> 196 us (0.947); the launches traced: 206 us -> 192 us
  waiting for transfers between devices: 49.6 us -> 40.4 us
  local copies, waits for them, and re-layouts: 9.8 us -> 2.86 us
  Pallas kernels: 25 us -> 28.7 us
  blocking collectives: 87.7 us -> 84.5 us
    ppermute x7, waiting for transfers between devices: 25.3 us -> 14 us  [reach(): return lax.ppermute(value, GROUP, [(at, at ^ step) for at in range(8)])]
    unnamed x24 -> x10, local copies, waits for them, and re-layouts: 9.47 us -> 2.53 us
    pallas_call x12 -> x13, Pallas kernels: 25 us -> 28.7 us  [call(): pl.pallas_call(kernel, out_shape=[jax.ShapeDtypeStruct(s, jnp.float32) fo...]
    all_to_all x4, blocking collectives: 87.7 us -> 84.5 us  [spread(): return lax.all_to_all(value, axes, 0, 0, tiled=True)]
  transfers between devices with their start and end apart: 14 -> 14, of which waited for: 7 -> 7; matrix products, arithmetic and copies ran while one was open for 0% -> 0% of each run, Pallas kernels for 7% -> 8%
where the time goes in v2:
time: 196 us; the launch traced here: 192 us
  blocking collectives  84.5 us (43%)
  waiting for transfers between devices  40.4 us (21%)
  starting transfers between devices  33.1 us (17%)
  Pallas kernels  28.7 us (15%)
  local copies, waits for them, and re-layouts  2.86 us (1%)
  other arithmetic  2.23 us (1%)
    all_to_all x4, blocking collectives, spread(): return lax.all_to_all(value, axes, 0, 0, tiled=True)  84.5 us
    pallas_call x13, Pallas kernels, call(): pl.pallas_call(kernel, out_shape=[jax.ShapeDtypeStruct(s, jnp.float32) fo...  28.7 us
    ppermute x7, waiting for transfers between devices, reach(): return lax.ppermute(value, GROUP, [(at, at ^ step) for at in range(8)])  14 us
    all_to_all x3, waiting for transfers between devices, spread(): return lax.all_to_all(value, axes, 0, 0, tiled=True)  13.5 us
    ppermute x4, waiting for transfers between devices, exchange(): return lax.ppermute(value, axis, [(0, 1), (1, 0)])  12.9 us
    all_to_all x3, starting transfers between devices, spread(): return lax.all_to_all(value, axes, 0, 0, tiled=True)  11.9 us
    ppermute x4, starting transfers between devices, exchange(): return lax.ppermute(value, axis, [(0, 1), (1, 0)])  11.4 us
    ppermute x7, starting transfers between devices, reach(): return lax.ppermute(value, GROUP, [(at, at ^ step) for at in range(8)])  9.74 us
  transfers between devices with their start and end apart: 14, of which 7 were waited for; matrix products, arithmetic and copies ran while one was open for 0% of the time, Pallas kernels for 8%

profile of v2, /device:TPU:1, one launch (start us, length us, event | category | flops | bytes accessed | tf_op | source)
XLA Modules:
  0.0 192.0 jit_solution(3712485694503050745)
XLA Ops:
  2.4 43.4 %all_to_all.35.a_ref = f32[16,11,8,512]{3,2,1,0:T(8,128)S(1)} all-to-all(f32[16,11,8,512]{3,2,1,0:T(8,128)S(1)} %bitcast.10), channel_id=1, replica_groups=mesh['zt'=2,'z1'=2,'z0'=2,'core'=2,'yh'=2,'yl'=2,'x'=4] {'yh','yl','x'}, dimensions={0} | all-to-all | bytes 5767168 | tf_op jit(solution)/shard_map/all_to_all | solution.py:245
  47.9 2.5 %collective-permute-start.5 = (f32[6,16,640]{2,1,0:T(8,128)S(1)}, f32[6,16,640]{2,1,0:T(8,128)S(1)}, u32[]{:S(2)}, u32[]{:S(2)}) collective-permute-start(f32[6,16,640]{2,1,0:T(8,128)S(1)} %get-tuple-element.36), channel_id=1, source_target_pairs={{0,6},{1,7},{2,4},{3,5},{4,2},{5,3},{6,0},{7,1},{8,14},{9,15},{10,... | collective-permute-start | bytes 737288 | tf_op jit(solution)/shard_map/ppermute | solution.py:241
  52.7 3.2 %collective-permute-start.6 = (f32[6,16,640]{2,1,0:T(8,128)S(1)}, f32[6,16,640]{2,1,0:T(8,128)S(1)}, u32[]{:S(2)}, u32[]{:S(2)}) collective-permute-start(f32[6,16,640]{2,1,0:T(8,128)S(1)} %get-tuple-element.37), channel_id=1, source_target_pairs={{0,7},{1,6},{2,5},{3,4},{4,3},{5,2},{6,1},{7,0},{8,15},{9,14},{10,... | collective-permute-start | bytes 737288 | tf_op jit(solution)/shard_map/ppermute | solution.py:241
  55.9 2.6 %shard_map.28 = (f32[6,16,640]{2,1,0:T(8,128)S(1)}, f32[6,16,640]{2,1,0:T(8,128)S(1)}, f32[6,16,640]{2,1,0:T(8,128)S(1)}, f32[6,16,640]{2,1,0:T(8,128)S(1)}) custom-call(s32[3]{0:T(128)S(1)} %pad_add_fusion.ids_ref, f32[16,11,8,512]{3,2,1,0:T(8,128)S(1)} %all_to_all.35.a_ref), custom_call_target="tpu_custom_call" | custom-call | flops 1000000000 | bytes 1000000 | tf_op jit(solution)/shard_map/pallas_call | solution.py:223
  62.5 9.8 %collective-permute-done.3 = f32[6,16,640]{2,1,0:T(8,128)S(1)} collective-permute-done((f32[6,16,640]{2,1,0:T(8,128)S(1)}, f32[6,16,640]{2,1,0:T(8,128)S(1)}, u32[]{:S(2)}, u32[]{:S(2)}) %collective-permute-start.3) | collective-permute-done | bytes 245792 | tf_op jit(solution)/shard_map/ppermute | solution.py:241
  72.4 3.9 %collective-permute-done.2 = f32[6,16,640]{2,1,0:T(8,128)S(1)} collective-permute-done((f32[6,16,640]{2,1,0:T(8,128)S(1)}, f32[6,16,640]{2,1,0:T(8,128)S(1)}, u32[]{:S(2)}, u32[]{:S(2)}) %collective-permute-start.2) | collective-permute-done | bytes 245792 | tf_op jit(solution)/shard_map/ppermute | solution.py:241
  76.4 13.0 %all_to_all.36.ag_ref = f32[8,2,16,640]{3,2,1,0:T(8,128)S(1)} all-to-all(f32[8,2,16,640]{3,2,1,0:T(8,128)S(1)} %broadcast_in_dim.3), channel_id=1, replica_groups=mesh['zt'=2,'z1'=2,'z0'=2,'core'=2,'yh'=2,'yl'=2,'x'=4] {'yl','x'}, dimensions={0} | all-to-all | bytes 1310720 | tf_op jit(solution)/shard_map/all_to_all | solution.py:245
  89.4 3.2 %shard_map.31 = (f32[2,5,16,128]{3,2,1,0:T(8,128)S(1)}, f32[16,16,512]{2,1,0:T(8,128)}, f32[4,16,512]{2,1,0:T(8,128)S(1)}) custom-call(s32[3]{0:T(128)S(1)} %pad_add_fusion.ids_ref, f32[8,2,16,640]{3,2,1,0:T(8,128)S(1)} %all_to_all.36.ag_ref, f32[6,16,640]{2,1,0:T(8,128)S(1)} %add_add_fusion.1.own_ref, f32[6,16,640]{2,1,0:T(8,128)S(1)} %add_add_fusion.other_ref), custom_call_target="tpu_custom_call" | custom-call | flops 100000000 | bytes 1000000 | tf_op jit(solution)/shard_map/pallas_call | solution.py:223
  92.6 4.1 %all-to-all-start.2 = ((f32[16,16,512]{2,1,0:T(8,128)}), f32[16,16,512]{2,1,0:T(8,128)S(1)}, u32[]{:S(2)}, u32[]{:S(2)}) async-start(f32[16,16,512]{2,1,0:T(8,128)} %get-tuple-element.38), calls=%async_computation.2 | async-start | bytes 1048576 | tf_op jit(solution)/shard_map/all_to_all | solution.py:245
  96.7 2.9 %collective-permute-start.7 = (f32[4,16,512]{2,1,0:T(8,128)S(1)}, f32[4,16,512]{2,1,0:T(8,128)S(1)}, u32[]{:S(2)}, u32[]{:S(2)}) collective-permute-start(f32[4,16,512]{2,1,0:T(8,128)S(1)} %get-tuple-element.39.own_ref), channel_id=1, source_target_pairs={{0,8},{8,0},{1,9},{9,1},{2,10},{10,2},{3,11},{11,3},{4,12},{12,4},... | collective-permute-start | bytes 393224 | tf_op jit(solution)/shard_map/ppermute | solution.py:235
  99.6 6.5 %all-to-all-done.2.ag_ref = f32[16,16,512]{2,1,0:T(8,128)S(1)} async-done(((f32[16,16,512]{2,1,0:T(8,128)}), f32[16,16,512]{2,1,0:T(8,128)S(1)}, u32[]{:S(2)}, u32[]{:S(2)}) %all-to-all-start.2) | async-done | bytes 524320 | tf_op jit(solution)/shard_map/all_to_all | solution.py:245
  109.7 14.4 %all_to_all.37.own_ref = f32[8,4,16,384]{3,2,1,0:T(8,128)S(1)} all-to-all(f32[8,4,16,384]{3,2,1,0:T(8,128)S(1)} %get-tuple-element.42), channel_id=1, replica_groups=mesh['zt'=2,'z1'=2,'z0'=2,'core'=2,'yh'=2,'yl'=2,'x'=4] {'yl','x'}, dimensions={0} | all-to-all | bytes 1572864 | tf_op jit(solution)/shard_map/all_to_all | solution.py:245
  124.2 3.5 %collective-permute-start.8 = (f32[8,4,16,384]{3,2,1,0:T(8,128)S(1)}, f32[8,4,16,384]{3,2,1,0:T(8,128)S(1)}, u32[]{:S(2)}, u32[]{:S(2)}) collective-permute-start(f32[8,4,16,384]{3,2,1,0:T(8,128)S(1)} %all_to_all.37.own_ref), channel_id=1, source_target_pairs={{0,16},{16,0},{1,17},{17,1},{2,18},{18,2},{3,19},{19,3},{4,20},{20... | collective-permute-start | bytes 2359304 | tf_op jit(solution)/shard_map/ppermute | solution.py:235
  127.7 3.5 %all-to-all-start.3 = ((f32[8,9,16,128]{3,2,1,0:T(8,128)}), f32[8,9,16,128]{3,2,1,0:T(8,128)S(1)}, u32[]{:S(2)}, u32[]{:S(2)}) async-start(f32[8,9,16,128]{3,2,1,0:T(8,128)} %get-tuple-element.41), calls=%async_computation.3 | async-start | bytes 1179648 | tf_op jit(solution)/shard_map/all_to_all | solution.py:245
  131.2 3.2 %shard_map.34 = (f32[384,128]{1,0:T(8,128)S(1)}, f32[384,256]{1,0:T(8,128)S(1)}) custom-call(f32[8,4,16,384]{3,2,1,0:T(8,128)S(1)} %all_to_all.37.own_ref, f32[8,4,16,384]{3,2,1,0:T(8,128)S(1)} %collective-permute-done.8.other_ref), custom_call_target="tpu_custom_call" | custom-call | flops 100000000 | bytes 1000000 | tf_op jit(solution)/shard_map/pallas_call | solution.py:223
  135.1 7.0 %all-to-all-done.3.x01_ref = f32[8,9,16,128]{3,2,1,0:T(8,128)S(1)} async-done(((f32[8,9,16,128]{3,2,1,0:T(8,128)}), f32[8,9,16,128]{3,2,1,0:T(8,128)S(1)}, u32[]{:S(2)}, u32[]{:S(2)}) %all-to-all-start.3) | async-done | bytes 589856 | tf_op jit(solution)/shard_map/all_to_all | solution.py:245
  142.9 5.4 %shard_map.35 = (f32[16,3,8,512]{3,2,1,0:T(8,128)}, f32[16,2,8,512]{3,2,1,0:T(8,128)}) custom-call(f32[16,11,8,512]{3,2,1,0:T(8,128)} %copy-done, f32[8,9,16,128]{3,2,1,0:T(8,128)} %copy-done.4, f32[384,128]{1,0:T(8,128)} %copy-done.3), custom_call_target="tpu_custom_call" | custom-call | flops 100000000 | bytes 1000000 | tf_op jit(solution)/shard_map/pallas_call | solution.py:223
  148.4 4.3 %all-to-all-start.5 = ((f32[16,3,8,512]{3,2,1,0:T(8,128)}), f32[16,3,8,512]{3,2,1,0:T(8,128)S(1)}, u32[]{:S(2)}, u32[]{:S(2)}) async-start(f32[16,3,8,512]{3,2,1,0:T(8,128)} %get-tuple-element.44.o_ref), calls=%async_computation.5 | async-start | bytes 1572864 | tf_op jit(solution)/shard_map/all_to_all | solution.py:245
  152.7 2.6 %collective-permute-start.9 = (f32[384,256]{1,0:T(8,128)S(1)}, f32[384,256]{1,0:T(8,128)S(1)}, u32[]{:S(2)}, u32[]{:S(2)}) collective-permute-start(f32[384,256]{1,0:T(8,128)S(1)} %get-tuple-element.46.own_ref), channel_id=1, source_target_pairs={{0,32},{32,0},{1,33},{33,1},{2,34},{34,2},{3,35},{35,3},{4,36},{36... | collective-permute-start | bytes 1179656 | tf_op jit(solution)/shard_map/ppermute | solution.py:235
  155.3 8.8 %collective-permute-done.9.other_ref = f32[384,256]{1,0:T(8,128)S(1)} collective-permute-done((f32[384,256]{1,0:T(8,128)S(1)}, f32[384,256]{1,0:T(8,128)S(1)}, u32[]{:S(2)}, u32[]{:S(2)}) %collective-permute-start.9) | collective-permute-done | bytes 393248 | tf_op jit(solution)/shard_map/ppermute | solution.py:235
  164.0 2.7 %shard_map.36 = (f32[256,128]{1,0:T(8,128)S(1)}, f32[256,128]{1,0:T(8,128)S(1)}) custom-call(f32[384,256]{1,0:T(8,128)S(1)} %get-tuple-element.46.own_ref, f32[384,256]{1,0:T(8,128)S(1)} %collective-permute-done.9.other_ref), custom_call_target="tpu_custom_call" | custom-call | flops 100000000 | bytes 1000000 | tf_op jit(solution)/shard_map/pallas_call | solution.py:223
  166.7 2.5 %collective-permute-start.10 = (f32[256,128]{1,0:T(8,128)S(1)}, f32[256,128]{1,0:T(8,128)S(1)}, u32[]{:S(2)}, u32[]{:S(2)}) collective-permute-start(f32[256,128]{1,0:T(8,128)S(1)} %get-tuple-element.48.own_ref), channel_id=1, source_target_pairs={{0,64},{64,0},{1,65},{65,1},{2,66},{66,2},{3,67},{67,3},{4,68},{68... | collective-permute-start | bytes 393224 | tf_op jit(solution)/shard_map/ppermute | solution.py:235
  170.8 4.2 %collective-permute-done.10.other_ref = f32[256,128]{1,0:T(8,128)S(1)} collective-permute-done((f32[256,128]{1,0:T(8,128)S(1)}, f32[256,128]{1,0:T(8,128)S(1)}, u32[]{:S(2)}, u32[]{:S(2)}) %collective-permute-start.10) | collective-permute-done | bytes 131104 | tf_op jit(solution)/shard_map/ppermute | solution.py:235
  177.2 13.7 %all_to_all.38.late_ref = f32[16,2,8,512]{3,2,1,0:T(8,128)S(1)} all-to-all(f32[16,2,8,512]{3,2,1,0:T(8,128)S(1)} %shard_map.39), channel_id=1, replica_groups=mesh['zt'=2,'z1'=2,'z0'=2,'core'=2,'yh'=2,'yl'=2,'x'=4] {'yh','yl','x'}, dimensions={0} | all-to-all | bytes 1048576 | tf_op jit(solution)/shard_map/all_to_all | solution.py:245
  (40 shorter events, 21.0 us)
Async XLA Ops:
  45.8 10.1 %copy-start = (f32[16,11,8,512]{3,2,1,0:T(8,128)}, f32[16,11,8,512]{3,2,1,0:T(8,128)S(1)}, u32[]{:S(2)}) copy-start(f32[16,11,8,512]{3,2,1,0:T(8,128)S(1)} %all_to_all.35.a_ref) | copy-start | bytes 8650756
  47.8 10.9 %collective-permute-start.4 = (f32[6,16,640]{2,1,0:T(8,128)S(1)}, f32[6,16,640]{2,1,0:T(8,128)S(1)}, u32[]{:S(2)}, u32[]{:S(2)}) collective-permute-start(f32[6,16,640]{2,1,0:T(8,128)S(1)} %get-tuple-element.35), channel_id=1, source_target_pairs={{0,5},{1,4},{2,7},{3,6},{4,1},{5,0},{6,3},{7,2},{8,13},{9,12},{10,... | collective-permute-start | bytes 737288 | tf_op jit(solution)/shard_map/ppermute | solution.py:241
  47.9 12.7 %collective-permute-start.5 = (f32[6,16,640]{2,1,0:T(8,128)S(1)}, f32[6,16,640]{2,1,0:T(8,128)S(1)}, u32[]{:S(2)}, u32[]{:S(2)}) collective-permute-start(f32[6,16,640]{2,1,0:T(8,128)S(1)} %get-tuple-element.36), channel_id=1, source_target_pairs={{0,6},{1,7},{2,4},{3,5},{4,2},{5,3},{6,0},{7,1},{8,14},{9,15},{10,... | collective-permute-start | bytes 737288 | tf_op jit(solution)/shard_map/ppermute | solution.py:241
  52.4 19.9 %collective-permute-start.3 = (f32[6,16,640]{2,1,0:T(8,128)S(1)}, f32[6,16,640]{2,1,0:T(8,128)S(1)}, u32[]{:S(2)}, u32[]{:S(2)}) collective-permute-start(f32[6,16,640]{2,1,0:T(8,128)S(1)} %get-tuple-element.34), channel_id=1, source_target_pairs={{0,4},{1,5},{2,6},{3,7},{4,0},{5,1},{6,2},{7,3},{8,12},{9,13},{10,... | collective-permute-start | bytes 737288 | tf_op jit(solution)/shard_map/ppermute | solution.py:241
  52.7 19.6 %collective-permute-start.6 = (f32[6,16,640]{2,1,0:T(8,128)S(1)}, f32[6,16,640]{2,1,0:T(8,128)S(1)}, u32[]{:S(2)}, u32[]{:S(2)}) collective-permute-start(f32[6,16,640]{2,1,0:T(8,128)S(1)} %get-tuple-element.37), channel_id=1, source_target_pairs={{0,7},{1,6},{2,5},{3,4},{4,3},{5,2},{6,1},{7,0},{8,15},{9,14},{10,... | collective-permute-start | bytes 737288 | tf_op jit(solution)/shard_map/ppermute | solution.py:241
  58.5 13.8 %collective-permute-start = (f32[6,16,640]{2,1,0:T(8,128)S(1)}, f32[6,16,640]{2,1,0:T(8,128)S(1)}, u32[]{:S(2)}, u32[]{:S(2)}) collective-permute-start(f32[6,16,640]{2,1,0:T(8,128)S(1)} %get-tuple-element.31), channel_id=1, source_target_pairs={{0,1},{1,0},{2,3},{3,2},{4,5},{5,4},{6,7},{7,6},{8,9},{9,8},{10,11... | collective-permute-start | bytes 737288 | tf_op jit(solution)/shard_map/ppermute | solution.py:241
  58.6 13.7 %collective-permute-start.1 = (f32[6,16,640]{2,1,0:T(8,128)S(1)}, f32[6,16,640]{2,1,0:T(8,128)S(1)}, u32[]{:S(2)}, u32[]{:S(2)}) collective-permute-start(f32[6,16,640]{2,1,0:T(8,128)S(1)} %get-tuple-element.32), channel_id=1, source_target_pairs={{0,2},{1,3},{2,0},{3,1},{4,6},{5,7},{6,4},{7,5},{8,10},{9,11},{10,... | collective-permute-start | bytes 737288 | tf_op jit(solution)/shard_map/ppermute | solution.py:241
  60.5 15.7 %collective-permute-start.2 = (f32[6,16,640]{2,1,0:T(8,128)S(1)}, f32[6,16,640]{2,1,0:T(8,128)S(1)}, u32[]{:S(2)}, u32[]{:S(2)}) collective-permute-start(f32[6,16,640]{2,1,0:T(8,128)S(1)} %get-tuple-element.33), channel_id=1, source_target_pairs={{0,3},{1,2},{2,1},{3,0},{4,7},{5,6},{6,5},{7,4},{8,11},{9,10},{10,... | collective-permute-start | bytes 737288 | tf_op jit(solution)/shard_map/ppermute | solution.py:241
  92.6 13.4 %all-to-all-start.2 = ((f32[16,16,512]{2,1,0:T(8,128)}), f32[16,16,512]{2,1,0:T(8,128)S(1)}, u32[]{:S(2)}, u32[]{:S(2)}) async-start(f32[16,16,512]{2,1,0:T(8,128)} %get-tuple-element.38), calls=%async_computation.2 | async-start | bytes 1048576 | tf_op jit(solution)/shard_map/all_to_all | solution.py:245
  96.7 10.9 %collective-permute-start.7 = (f32[4,16,512]{2,1,0:T(8,128)S(1)}, f32[4,16,512]{2,1,0:T(8,128)S(1)}, u32[]{:S(2)}, u32[]{:S(2)}) collective-permute-start(f32[4,16,512]{2,1,0:T(8,128)S(1)} %get-tuple-element.39.own_ref), channel_id=1, source_target_pairs={{0,8},{8,0},{1,9},{9,1},{2,10},{10,2},{3,11},{11,3},{4,12},{12,4},... | collective-permute-start | bytes 393224 | tf_op jit(solution)/shard_map/ppermute | solution.py:235
  124.2 7.0 %collective-permute-start.8 = (f32[8,4,16,384]{3,2,1,0:T(8,128)S(1)}, f32[8,4,16,384]{3,2,1,0:T(8,128)S(1)}, u32[]{:S(2)}, u32[]{:S(2)}) collective-permute-start(f32[8,4,16,384]{3,2,1,0:T(8,128)S(1)} %all_to_all.37.own_ref), channel_id=1, source_target_pairs={{0,16},{16,0},{1,17},{17,1},{2,18},{18,2},{3,19},{19,3},{4,20},{20... | collective-permute-start | bytes 2359304 | tf_op jit(solution)/shard_map/ppermute | solution.py:235
  127.7 14.4 %all-to-all-start.3 = ((f32[8,9,16,128]{3,2,1,0:T(8,128)}), f32[8,9,16,128]{3,2,1,0:T(8,128)S(1)}, u32[]{:S(2)}, u32[]{:S(2)}) async-start(f32[8,9,16,128]{3,2,1,0:T(8,128)} %get-tuple-element.41), calls=%async_computation.3 | async-start | bytes 1179648 | tf_op jit(solution)/shard_map/all_to_all | solution.py:245
  134.4 0.7 copy-start.3
  142.1 0.8 copy-start.4
  148.3 20.8 %copy-start.1 = (f32[16,3,8,512]{3,2,1,0:T(8,128)S(1)}, f32[16,3,8,512]{3,2,1,0:T(8,128)}, u32[]{:S(2)}) copy-start(f32[16,3,8,512]{3,2,1,0:T(8,128)} %get-tuple-element.44.o_ref) | copy-start | bytes 2359300
  148.4 28.8 %all-to-all-start.5 = ((f32[16,3,8,512]{3,2,1,0:T(8,128)}), f32[16,3,8,512]{3,2,1,0:T(8,128)S(1)}, u32[]{:S(2)}, u32[]{:S(2)}) async-start(f32[16,3,8,512]{3,2,1,0:T(8,128)} %get-tuple-element.44.o_ref), calls=%async_computation.5 | async-start | bytes 1572864 | tf_op jit(solution)/shard_map/all_to_all | solution.py:245
  152.7 11.3 %collective-permute-start.9 = (f32[384,256]{1,0:T(8,128)S(1)}, f32[384,256]{1,0:T(8,128)S(1)}, u32[]{:S(2)}, u32[]{:S(2)}) collective-permute-start(f32[384,256]{1,0:T(8,128)S(1)} %get-tuple-element.46.own_ref), channel_id=1, source_target_pairs={{0,32},{32,0},{1,33},{33,1},{2,34},{34,2},{3,35},{35,3},{4,36},{36... | collective-permute-start | bytes 1179656 | tf_op jit(solution)/shard_map/ppermute | solution.py:235
  166.7 8.2 %collective-permute-start.10 = (f32[256,128]{1,0:T(8,128)S(1)}, f32[256,128]{1,0:T(8,128)S(1)}, u32[]{:S(2)}, u32[]{:S(2)}) collective-permute-start(f32[256,128]{1,0:T(8,128)S(1)} %get-tuple-element.48.own_ref), channel_id=1, source_target_pairs={{0,64},{64,0},{1,65},{65,1},{2,66},{66,2},{3,67},{67,3},{4,68},{68... | collective-permute-start | bytes 393224 | tf_op jit(solution)/shard_map/ppermute | solution.py:235
  169.2 1.0 copy-start.2

commit v3 on v2

--- a/solution.py
+++ b/solution.py
@@ -136,30 +136,34 @@
     inverse(dot(p1[:, :K], p2[:, :K]), x_ref, r_ref)
 
 
-def level1_kernel(ids_ref, ag_ref, own_ref, other_ref, x0_ref, inverse_ref, x_out, s_out):
+def level1_kernel(ids_ref, ag_ref, own_ref, other_ref, x0_ref, inverse_ref, s_out):
     width = (LEVELS - 2) * K
     n = LEVELS - 2
     p1, p2 = level1_panels(ids_ref, ag_ref)
     own, other = own_ref[...].reshape(n * 16, width), other_ref[...].reshape(n * 16, width)
     target = other[:, :K] - dot(own[:, :K], p2[:, :K])
     x1, _, state = substitute(p1, p2, own, other, target, inverse_ref)
+    state = state.reshape(n, 16, width - K)
+    for m in range(n):
+        for level in range(3):
+            block = state[m, :, level * K : (level + 1) * K]
+            s_out[:, 3 * m + level] = jnp.broadcast_to(block, (8, 16, K))
     half = (4, n + 1, 16, K)
-    x_out[:4, : n + 1] = jnp.broadcast_to(x0_ref[0], half)
-    x_out[4:, : n + 1] = jnp.broadcast_to(x0_ref[1], half)
-    x_out[:, n + 1 :] = jnp.broadcast_to(x1.reshape(n, 16, K), (8, n, 16, K))
-    s_out[...] = jnp.broadcast_to(state.reshape(n, 16, width - K), s_out.shape)
+    s_out[:4, 12:17] = jnp.broadcast_to(x0_ref[0], half)
+    s_out[4:, 12:17] = jnp.broadcast_to(x0_ref[1], half)
+    s_out[:, 17:] = jnp.broadcast_to(x1.reshape(n, 16, K), (8, n, 16, K))
 
 
 def level2_kernel(own_ref, other_ref, x_out, s_out, x_ref, r_ref):
-    width = (LEVELS - 3) * K
     n = LEVELS - 3
 
+    def member(ref, m):
+        return jnp.concatenate([ref[:, 3 * m + level].reshape(K, K) for level in range(3)], axis=1)
+
     def rest(ref):
-        return jnp.concatenate([ref[:, m].reshape(K, width) for m in range(1, n + 1)], axis=0)
-
-    x1, _, state = eliminate(
-        own_ref[:, 0].reshape(K, width), other_ref[:, 0].reshape(K, width), rest(own_ref), rest(other_ref), x_ref, r_ref
-    )
+        return jnp.concatenate([member(ref, m) for m in range(1, n + 1)], axis=0)
+
+    x1, _, state = eliminate(member(own_ref, 0), member(other_ref, 0), rest(own_ref), rest(other_ref), x_ref, r_ref)
     x_out[...] = x1
     s_out[...] = state
 
@@ -181,7 +185,7 @@
     def factor(level, i):
         if level == 2:
             return x2_ref[i * K : (i + 1) * K]
-        return x01_ref[:, (LEVELS - 1) * level + i].reshape(K, K)
+        return x01_ref[:, 12 + (LEVELS - 1) * level + i].reshape(K, K)
 
     for m in range(1, LEVELS):
         value = a_ref[:, m].reshape(K, -1)
@@ -267,15 +271,13 @@
     other = exchange(rest, "yh")
     panels = spread(panel, COLS)
     (inv,) = call(level1_inverse_kernel, [(K, K)], ids, panels, scalar=True)
-    outs = [(8, 9, 16, K), (8, 4, 16, 3 * K)]
-    x01, s1 = call(level1_kernel, outs, ids, panels, rest, other, x0, inv, scalar=True)
+    (s1,) = call(level1_kernel, [(8, 21, 16, K)], ids, panels, rest, other, x0, inv, scalar=True)
 
     s1 = spread(s1, GROUP)
-    other = exchange(s1, "core")
-    x01 = spread(x01, GROUP)
+    other = exchange(s1[:, :12], "core")
     x2, s2 = call(level2_kernel, [(3 * K, K), (3 * K, 2 * K)], s1, other)
     other = exchange(s2, "z0")
-    early, part = call(finish_kernel, [(16, 3, 8, 512), (16, 2, 8, 512)], rows, x01, x2)
+    early, part = call(finish_kernel, [(16, 3, 8, 512), (16, 2, 8, 512)], rows, s1, x2)
     early_out = spread(early, COLS)
     x3, s3 = call(level3_kernel, [(2 * K, K), (2 * K, K)], s2, other)
     other = exchange(s3, "z1")
@@ -305,7 +307,7 @@
     level2_kernel=12,
     level3_kernel=12,
     level4_kernel=12,
-    finish_kernel=58,
+    finish_kernel=24,
     later_kernel=12,
     last_kernel=12,
 )

time: 196 us -> 196 us (level); the launches traced: 192 us -> 196 us
  blocking collectives: 84.5 us -> 93.8 us
  Pallas kernels: 28.7 us -> 24.8 us
  starting transfers between devices: 33.1 us -> 30.2 us
  local copies, waits for them, and re-layouts: 2.86 us -> 5.46 us
    all_to_all x4, blocking collectives: 84.5 us -> 93.8 us  [spread(): return lax.all_to_all(value, axes, 0, 0, tiled=True)]
    all_to_all x3 -> x2, waiting for transfers between devices: 13.5 us -> 6.49 us  [spread(): return lax.all_to_all(value, axes, 0, 0, tiled=True)]
    pallas_call x13, Pallas kernels: 28.7 us -> 24.8 us  [call(): pl.pallas_call(kernel, out_shape=[jax.ShapeDtypeStruct(s, jnp.float32) fo...]
    all_to_all x3 -> x2, starting transfers between devices: 11.9 us -> 8.15 us  [spread(): return lax.all_to_all(value, axes, 0, 0, tiled=True)]
    ppermute x7, waiting for transfers between devices: 14 us -> 17.7 us  [reach(): return lax.ppermute(value, GROUP, [(at, at ^ step) for at in range(8)])]
    unnamed x10 -> x14, local copies, waits for them, and re-layouts: 2.53 us -> 5.06 us
    ppermute x4, waiting for transfers between devices: 12.9 us -> 14.9 us  [exchange(): return lax.ppermute(value, axis, [(0, 1), (1, 0)])]
  transfers between devices with their start and end apart: 14 -> 13, of which waited for: 7 -> 8; matrix products, arithmetic and copies ran while one was open for 0% -> 0% of each run, Pallas kernels for 8% -> 6%
where the time goes in v3:
time: 196 us
  blocking collectives  93.8 us (48%)
  waiting for transfers between devices  39.1 us (20%)
  starting transfers between devices  30.2 us (15%)
  Pallas kernels  24.8 us (13%)
  local copies, waits for them, and re-layouts  5.46 us (3%)
  other arithmetic  2.2 us (1%)
    all_to_all x4, blocking collectives, spread(): return lax.all_to_all(value, axes, 0, 0, tiled=True)  93.8 us
    pallas_call x13, Pallas kernels, call(): pl.pallas_call(kernel, out_shape=[jax.ShapeDtypeStruct(s, jnp.float32) fo...  24.8 us
    ppermute x7, waiting for transfers between devices, reach(): return lax.ppermute(value, GROUP, [(at, at ^ step) for at in range(8)])  17.7 us
    ppermute x4, waiting for transfers between devices, exchange(): return lax.ppermute(value, axis, [(0, 1), (1, 0)])  14.9 us
    ppermute x4, starting transfers between devices, exchange(): return lax.ppermute(value, axis, [(0, 1), (1, 0)])  12.4 us
    ppermute x7, starting transfers between devices, reach(): return lax.ppermute(value, GROUP, [(at, at ^ step) for at in range(8)])  9.65 us
    all_to_all x2, starting transfers between devices, spread(): return lax.all_to_all(value, axes, 0, 0, tiled=True)  8.15 us
    all_to_all x2, waiting for transfers between devices, spread(): return lax.all_to_all(value, axes, 0, 0, tiled=True)  6.49 us
  transfers between devices with their start and end apart: 13, of which 8 were waited for; matrix products, arithmetic and copies ran while one was open for 0% of the time, Pallas kernels for 6%

profile of v3, /device:TPU:1, one launch (start us, length us, event | category | flops | bytes accessed | tf_op | source)
XLA Modules:
  0.0 195.8 jit_solution(12927765775074652684)
XLA Ops:
  0.1 2.0 %pad_maximum_fusion = f32[11,8,8192]{2,1,0:T(8,128)S(1)} fusion(f32[5,8,8192]{2,1,0:T(8,128)} %param.3, f32[6,8,8192]{2,1,0:T(8,128)} %param.2), kind=kLoop, calls=%fused_computation.1 | loop fusion | flops 720896 | bytes 5767168 | tf_op jit(solution)/shard_map/concatenate | solution.py:255
  2.4 43.4 %all_to_all.30.a_ref = f32[16,11,8,512]{3,2,1,0:T(8,128)S(1)} all-to-all(f32[16,11,8,512]{3,2,1,0:T(8,128)S(1)} %bitcast.10), channel_id=1, replica_groups=mesh['zt'=2,'z1'=2,'z0'=2,'core'=2,'yh'=2,'yl'=2,'x'=4] {'yh','yl','x'}, dimensions={0} | all-to-all | bytes 5767168 | tf_op jit(solution)/shard_map/all_to_all | solution.py:249
  45.8 2.6 %shard_map.28 = (f32[6,16,640]{2,1,0:T(8,128)S(1)}, f32[6,16,640]{2,1,0:T(8,128)S(1)}, f32[6,16,640]{2,1,0:T(8,128)S(1)}, f32[6,16,640]{2,1,0:T(8,128)S(1)}) custom-call(s32[3]{0:T(128)S(1)} %pad_add_fusion.ids_ref, f32[16,11,8,512]{3,2,1,0:T(8,128)S(1)} %all_to_all.30.a_ref), custom_call_target="tpu_custom_call" | custom-call | flops 1000000000 | bytes 1000000 | tf_op jit(solution)/shard_map/pallas_call | solution.py:227
  50.1 2.2 %collective-permute-start.2 = (f32[6,16,640]{2,1,0:T(8,128)S(1)}, f32[6,16,640]{2,1,0:T(8,128)S(1)}, u32[]{:S(2)}, u32[]{:S(2)}) collective-permute-start(f32[6,16,640]{2,1,0:T(8,128)S(1)} %get-tuple-element.31), channel_id=1, source_target_pairs={{0,3},{1,2},{2,1},{3,0},{4,7},{5,6},{6,5},{7,4},{8,11},{9,10},{10,... | collective-permute-start | bytes 737288 | tf_op jit(solution)/shard_map/ppermute | solution.py:245
  54.4 2.5 %collective-permute-start.5 = (f32[6,16,640]{2,1,0:T(8,128)S(1)}, f32[6,16,640]{2,1,0:T(8,128)S(1)}, u32[]{:S(2)}, u32[]{:S(2)}) collective-permute-start(f32[6,16,640]{2,1,0:T(8,128)S(1)} %get-tuple-element.34), channel_id=1, source_target_pairs={{0,6},{1,7},{2,4},{3,5},{4,2},{5,3},{6,0},{7,1},{8,14},{9,15},{10,... | collective-permute-start | bytes 737288 | tf_op jit(solution)/shard_map/ppermute | solution.py:245
  59.7 2.8 %collective-permute-start.6 = (f32[6,16,640]{2,1,0:T(8,128)S(1)}, f32[6,16,640]{2,1,0:T(8,128)S(1)}, u32[]{:S(2)}, u32[]{:S(2)}) collective-permute-start(f32[6,16,640]{2,1,0:T(8,128)S(1)} %get-tuple-element.35), channel_id=1, source_target_pairs={{0,7},{1,6},{2,5},{3,4},{4,3},{5,2},{6,1},{7,0},{8,15},{9,14},{10,... | collective-permute-start | bytes 737288 | tf_op jit(solution)/shard_map/ppermute | solution.py:245
  63.3 7.5 %collective-permute-done.5 = f32[6,16,640]{2,1,0:T(8,128)S(1)} collective-permute-done((f32[6,16,640]{2,1,0:T(8,128)S(1)}, f32[6,16,640]{2,1,0:T(8,128)S(1)}, u32[]{:S(2)}, u32[]{:S(2)}) %collective-permute-start.5) | collective-permute-done | bytes 245792 | tf_op jit(solution)/shard_map/ppermute | solution.py:245
  70.8 9.1 %collective-permute-done.3 = f32[6,16,640]{2,1,0:T(8,128)S(1)} collective-permute-done((f32[6,16,640]{2,1,0:T(8,128)S(1)}, f32[6,16,640]{2,1,0:T(8,128)S(1)}, u32[]{:S(2)}, u32[]{:S(2)}) %collective-permute-start.3) | collective-permute-done | bytes 245792 | tf_op jit(solution)/shard_map/ppermute | solution.py:245
  80.0 13.6 %all_to_all.31.ag_ref = f32[8,2,16,640]{3,2,1,0:T(8,128)S(1)} all-to-all(f32[8,2,16,640]{3,2,1,0:T(8,128)S(1)} %broadcast_in_dim.3), channel_id=1, replica_groups=mesh['zt'=2,'z1'=2,'z0'=2,'core'=2,'yh'=2,'yl'=2,'x'=4] {'yl','x'}, dimensions={0} | all-to-all | bytes 1310720 | tf_op jit(solution)/shard_map/all_to_all | solution.py:249
  93.6 2.4 %shard_map.31 = (f32[2,5,16,128]{3,2,1,0:T(8,128)S(1)}, f32[16,16,512]{2,1,0:T(8,128)S(1)}, f32[4,16,512]{2,1,0:T(8,128)S(1)}) custom-call(s32[3]{0:T(128)S(1)} %pad_add_fusion.ids_ref, f32[8,2,16,640]{3,2,1,0:T(8,128)S(1)} %all_to_all.31.ag_ref, f32[6,16,640]{2,1,0:T(8,128)S(1)} %add_add_fusion.1.own_ref, f32[6,16,640]{2,1,0:T(8,128)S(1)} %add_add_fusion.other_ref), custom_call_target="tpu_custom_call" | custom-call | flops 100000000 | bytes 1000000 | tf_op jit(solution)/shard_map/pallas_call | solution.py:227
  97.4 3.6 %all-to-all-start.2 = ((f32[16,16,512]{2,1,0:T(8,128)}), f32[16,16,512]{2,1,0:T(8,128)S(1)}, u32[]{:S(2)}, u32[]{:S(2)}) async-start(f32[16,16,512]{2,1,0:T(8,128)} %copy-done.2), calls=%async_computation.2 | async-start | bytes 1048576 | tf_op jit(solution)/shard_map/all_to_all | solution.py:249
  101.0 2.8 %collective-permute-start.7 = (f32[4,16,512]{2,1,0:T(8,128)S(1)}, f32[4,16,512]{2,1,0:T(8,128)}, u32[]{:S(2)}, u32[]{:S(2)}) collective-permute-start(f32[4,16,512]{2,1,0:T(8,128)S(1)} %get-tuple-element.37.own_ref), channel_id=1, source_target_pairs={{0,8},{8,0},{1,9},{9,1},{2,10},{10,2},{3,11},{11,3},{4,12},{12,4},... | collective-permute-start | bytes 393224 | tf_op jit(solution)/shard_map/ppermute | solution.py:239
  103.8 6.5 %all-to-all-done.2.ag_ref = f32[16,16,512]{2,1,0:T(8,128)S(1)} async-done(((f32[16,16,512]{2,1,0:T(8,128)}), f32[16,16,512]{2,1,0:T(8,128)S(1)}, u32[]{:S(2)}, u32[]{:S(2)}) %all-to-all-start.2) | async-done | bytes 524320 | tf_op jit(solution)/shard_map/all_to_all | solution.py:249
  114.6 20.5 %all_to_all.32.own_ref.x01_ref = f32[8,21,16,128]{3,2,1,0:T(8,128)S(1)} all-to-all(f32[8,21,16,128]{3,2,1,0:T(8,128)S(1)} %shard_map.33), channel_id=1, replica_groups=mesh['zt'=2,'z1'=2,'z0'=2,'core'=2,'yh'=2,'yl'=2,'x'=4] {'yl','x'}, dimensions={0} | all-to-all | bytes 2752512 | tf_op jit(solution)/shard_map/all_to_all | solution.py:249
  135.2 3.9 %collective-permute-start.8 = (f32[8,12,16,128]{3,2,1,0:T(8,128)S(1)}, f32[8,12,16,128]{3,2,1,0:T(8,128)S(1)}, u32[]{:S(2)}, u32[]{:S(2)}) collective-permute-start(f32[8,12,16,128]{3,2,1,0:T(8,128)S(1)} %slice.14), channel_id=1, source_target_pairs={{0,16},{16,0},{1,17},{17,1},{2,18},{18,2},{3,19},{19,3},{4,20},{20... | collective-permute-start | bytes 2359304 | tf_op jit(solution)/shard_map/ppermute | solution.py:239
  141.0 3.2 %shard_map.34 = (f32[384,128]{1,0:T(8,128)S(1)}, f32[384,256]{1,0:T(8,128)S(1)}) custom-call(f32[8,21,16,128]{3,2,1,0:T(8,128)S(1)} %all_to_all.32.own_ref.x01_ref, f32[8,12,16,128]{3,2,1,0:T(8,128)S(1)} %collective-permute-done.8.other_ref), custom_call_target="tpu_custom_call" | custom-call | flops 100000000 | bytes 1000000 | tf_op jit(solution)/shard_map/pallas_call | solution.py:227
  145.0 2.6 %shard_map.35 = (f32[16,3,8,512]{3,2,1,0:T(8,128)S(1)}, f32[16,2,8,512]{3,2,1,0:T(8,128)S(1)}) custom-call(f32[16,11,8,512]{3,2,1,0:T(8,128)S(1)} %all_to_all.30.a_ref, f32[8,21,16,128]{3,2,1,0:T(8,128)S(1)} %all_to_all.32.own_ref.x01_ref, f32[384,128]{1,0:T(8,128)S(1)} %get-tuple-element.39.x2_ref), custom_call_target="tpu_custom_call" | custom-call | flops 100000000 | bytes 1000000 | tf_op jit(solution)/shard_map/pallas_call | solution.py:227
  148.5 4.6 %all-to-all-start.4 = ((f32[16,3,8,512]{3,2,1,0:T(8,128)}), f32[16,3,8,512]{3,2,1,0:T(8,128)S(1)}, u32[]{:S(2)}, u32[]{:S(2)}) async-start(f32[16,3,8,512]{3,2,1,0:T(8,128)} %copy-done), calls=%async_computation.4 | async-start | bytes 1572864 | tf_op jit(solution)/shard_map/all_to_all | solution.py:249
  153.1 2.6 %collective-permute-start.9 = (f32[384,256]{1,0:T(8,128)S(1)}, f32[384,256]{1,0:T(8,128)S(1)}, u32[]{:S(2)}, u32[]{:S(2)}) collective-permute-start(f32[384,256]{1,0:T(8,128)S(1)} %copy-done.4), channel_id=1, source_target_pairs={{0,32},{32,0},{1,33},{33,1},{2,34},{34,2},{3,35},{35,3},{4,36},{36... | collective-permute-start | bytes 1179656 | tf_op jit(solution)/shard_map/ppermute | solution.py:239
  155.6 8.8 %collective-permute-done.9.other_ref = f32[384,256]{1,0:T(8,128)S(1)} collective-permute-done((f32[384,256]{1,0:T(8,128)S(1)}, f32[384,256]{1,0:T(8,128)S(1)}, u32[]{:S(2)}, u32[]{:S(2)}) %collective-permute-start.9) | collective-permute-done | bytes 393248 | tf_op jit(solution)/shard_map/ppermute | solution.py:239
  164.5 2.6 %shard_map.36 = (f32[256,128]{1,0:T(8,128)S(1)}, f32[256,128]{1,0:T(8,128)S(1)}) custom-call(f32[384,256]{1,0:T(8,128)S(1)} %copy-done.4, f32[384,256]{1,0:T(8,128)S(1)} %collective-permute-done.9.other_ref), custom_call_target="tpu_custom_call" | custom-call | flops 100000000 | bytes 1000000 | tf_op jit(solution)/shard_map/pallas_call | solution.py:227
  167.1 3.1 %collective-permute-start.10 = (f32[256,128]{1,0:T(8,128)S(1)}, f32[256,128]{1,0:T(8,128)S(1)}, u32[]{:S(2)}, u32[]{:S(2)}) collective-permute-start(f32[256,128]{1,0:T(8,128)S(1)} %get-tuple-element.44.own_ref), channel_id=1, source_target_pairs={{0,64},{64,0},{1,65},{65,1},{2,66},{66,2},{3,67},{67,3},{4,68},{68... | collective-permute-start | bytes 393224 | tf_op jit(solution)/shard_map/ppermute | solution.py:239
  172.0 4.2 %collective-permute-done.10.other_ref = f32[256,128]{1,0:T(8,128)S(1)} collective-permute-done((f32[256,128]{1,0:T(8,128)S(1)}, f32[256,128]{1,0:T(8,128)S(1)}, u32[]{:S(2)}, u32[]{:S(2)}) %collective-permute-start.10) | collective-permute-done | bytes 131104 | tf_op jit(solution)/shard_map/ppermute | solution.py:239
  178.3 16.3 %all_to_all.33.late_ref = f32[16,2,8,512]{3,2,1,0:T(8,128)S(1)} all-to-all(f32[16,2,8,512]{3,2,1,0:T(8,128)S(1)} %shard_map.39), channel_id=1, replica_groups=mesh['zt'=2,'z1'=2,'z0'=2,'core'=2,'yh'=2,'yl'=2,'x'=4] {'yh','yl','x'}, dimensions={0} | all-to-all | bytes 1048576 | tf_op jit(solution)/shard_map/all_to_all | solution.py:249
  (43 shorter events, 22.1 us)
Async XLA Ops:
  48.4 10.6 %collective-permute-start = (f32[6,16,640]{2,1,0:T(8,128)S(1)}, f32[6,16,640]{2,1,0:T(8,128)S(1)}, u32[]{:S(2)}, u32[]{:S(2)}) collective-permute-start(f32[6,16,640]{2,1,0:T(8,128)S(1)} %get-tuple-element.29), channel_id=1, source_target_pairs={{0,1},{1,0},{2,3},{3,2},{4,5},{5,4},{6,7},{7,6},{8,9},{9,8},{10,11... | collective-permute-start | bytes 737288 | tf_op jit(solution)/shard_map/ppermute | solution.py:245
  48.8 10.9 %collective-permute-start.1 = (f32[6,16,640]{2,1,0:T(8,128)S(1)}, f32[6,16,640]{2,1,0:T(8,128)S(1)}, u32[]{:S(2)}, u32[]{:S(2)}) collective-permute-start(f32[6,16,640]{2,1,0:T(8,128)S(1)} %get-tuple-element.30), channel_id=1, source_target_pairs={{0,2},{1,3},{2,0},{3,1},{4,6},{5,7},{6,4},{7,5},{8,10},{9,11},{10,... | collective-permute-start | bytes 737288 | tf_op jit(solution)/shard_map/ppermute | solution.py:245
  50.1 12.3 %collective-permute-start.2 = (f32[6,16,640]{2,1,0:T(8,128)S(1)}, f32[6,16,640]{2,1,0:T(8,128)S(1)}, u32[]{:S(2)}, u32[]{:S(2)}) collective-permute-start(f32[6,16,640]{2,1,0:T(8,128)S(1)} %get-tuple-element.31), channel_id=1, source_target_pairs={{0,3},{1,2},{2,1},{3,0},{4,7},{5,6},{6,5},{7,4},{8,11},{9,10},{10,... | collective-permute-start | bytes 737288 | tf_op jit(solution)/shard_map/ppermute | solution.py:245
  54.3 9.0 %collective-permute-start.4 = (f32[6,16,640]{2,1,0:T(8,128)S(1)}, f32[6,16,640]{2,1,0:T(8,128)S(1)}, u32[]{:S(2)}, u32[]{:S(2)}) collective-permute-start(f32[6,16,640]{2,1,0:T(8,128)S(1)} %get-tuple-element.33), channel_id=1, source_target_pairs={{0,5},{1,4},{2,7},{3,6},{4,1},{5,0},{6,3},{7,2},{8,13},{9,12},{10,... | collective-permute-start | bytes 737288 | tf_op jit(solution)/shard_map/ppermute | solution.py:245
  54.4 16.3 %collective-permute-start.5 = (f32[6,16,640]{2,1,0:T(8,128)S(1)}, f32[6,16,640]{2,1,0:T(8,128)S(1)}, u32[]{:S(2)}, u32[]{:S(2)}) collective-permute-start(f32[6,16,640]{2,1,0:T(8,128)S(1)} %get-tuple-element.34), channel_id=1, source_target_pairs={{0,6},{1,7},{2,4},{3,5},{4,2},{5,3},{6,0},{7,1},{8,14},{9,15},{10,... | collective-permute-start | bytes 737288 | tf_op jit(solution)/shard_map/ppermute | solution.py:245
  59.0 20.9 %collective-permute-start.3 = (f32[6,16,640]{2,1,0:T(8,128)S(1)}, f32[6,16,640]{2,1,0:T(8,128)S(1)}, u32[]{:S(2)}, u32[]{:S(2)}) collective-permute-start(f32[6,16,640]{2,1,0:T(8,128)S(1)} %get-tuple-element.32), channel_id=1, source_target_pairs={{0,4},{1,5},{2,6},{3,7},{4,0},{5,1},{6,2},{7,3},{8,12},{9,13},{10,... | collective-permute-start | bytes 737288 | tf_op jit(solution)/shard_map/ppermute | solution.py:245
  59.7 20.2 %collective-permute-start.6 = (f32[6,16,640]{2,1,0:T(8,128)S(1)}, f32[6,16,640]{2,1,0:T(8,128)S(1)}, u32[]{:S(2)}, u32[]{:S(2)}) collective-permute-start(f32[6,16,640]{2,1,0:T(8,128)S(1)} %get-tuple-element.35), channel_id=1, source_target_pairs={{0,7},{1,6},{2,5},{3,4},{4,3},{5,2},{6,1},{7,0},{8,15},{9,14},{10,... | collective-permute-start | bytes 737288 | tf_op jit(solution)/shard_map/ppermute | solution.py:245
  96.0 0.8 copy-start.2
  96.8 0.6 copy-start.5
  97.4 12.9 %all-to-all-start.2 = ((f32[16,16,512]{2,1,0:T(8,128)}), f32[16,16,512]{2,1,0:T(8,128)S(1)}, u32[]{:S(2)}, u32[]{:S(2)}) async-start(f32[16,16,512]{2,1,0:T(8,128)} %copy-done.2), calls=%async_computation.2 | async-start | bytes 1048576 | tf_op jit(solution)/shard_map/all_to_all | solution.py:249
  101.0 10.9 %collective-permute-start.7 = (f32[4,16,512]{2,1,0:T(8,128)S(1)}, f32[4,16,512]{2,1,0:T(8,128)}, u32[]{:S(2)}, u32[]{:S(2)}) collective-permute-start(f32[4,16,512]{2,1,0:T(8,128)S(1)} %get-tuple-element.37.own_ref), channel_id=1, source_target_pairs={{0,8},{8,0},{1,9},{9,1},{2,10},{10,2},{3,11},{11,3},{4,12},{12,4},... | collective-permute-start | bytes 393224 | tf_op jit(solution)/shard_map/ppermute | solution.py:239
  111.9 0.9 copy-start.6
  135.2 5.8 %collective-permute-start.8 = (f32[8,12,16,128]{3,2,1,0:T(8,128)S(1)}, f32[8,12,16,128]{3,2,1,0:T(8,128)S(1)}, u32[]{:S(2)}, u32[]{:S(2)}) collective-permute-start(f32[8,12,16,128]{3,2,1,0:T(8,128)S(1)} %slice.14), channel_id=1, source_target_pairs={{0,16},{16,0},{1,17},{17,1},{2,18},{18,2},{3,19},{19,3},{4,20},{20... | collective-permute-start | bytes 2359304 | tf_op jit(solution)/shard_map/ppermute | solution.py:239
  144.2 0.8 copy-start.3
  147.6 0.9 copy-start
  148.5 4.6 %copy-start.4 = (f32[384,256]{1,0:T(8,128)S(1)}, f32[384,256]{1,0:T(8,128)}, u32[]{:S(2)}) copy-start(f32[384,256]{1,0:T(8,128)} %copy-done.3) | copy-start | bytes 1179652
  148.5 29.9 %all-to-all-start.4 = ((f32[16,3,8,512]{3,2,1,0:T(8,128)}), f32[16,3,8,512]{3,2,1,0:T(8,128)S(1)}, u32[]{:S(2)}, u32[]{:S(2)}) async-start(f32[16,3,8,512]{3,2,1,0:T(8,128)} %copy-done), calls=%async_computation.4 | async-start | bytes 1572864 | tf_op jit(solution)/shard_map/all_to_all | solution.py:249
  153.1 11.4 %collective-permute-start.9 = (f32[384,256]{1,0:T(8,128)S(1)}, f32[384,256]{1,0:T(8,128)S(1)}, u32[]{:S(2)}, u32[]{:S(2)}) collective-permute-start(f32[384,256]{1,0:T(8,128)S(1)} %copy-done.4), channel_id=1, source_target_pairs={{0,32},{32,0},{1,33},{33,1},{2,34},{34,2},{3,35},{35,3},{4,36},{36... | collective-permute-start | bytes 1179656 | tf_op jit(solution)/shard_map/ppermute | solution.py:239
  167.1 9.0 %collective-permute-start.10 = (f32[256,128]{1,0:T(8,128)S(1)}, f32[256,128]{1,0:T(8,128)S(1)}, u32[]{:S(2)}, u32[]{:S(2)}) collective-permute-start(f32[256,128]{1,0:T(8,128)S(1)} %get-tuple-element.44.own_ref), channel_id=1, source_target_pairs={{0,64},{64,0},{1,65},{65,1},{2,66},{66,2},{3,67},{67,3},{4,68},{68... | collective-permute-start | bytes 393224 | tf_op jit(solution)/shard_map/ppermute | solution.py:239
  170.2 1.1 copy-start.1
